TPU v7x, 32 devices: a 4x4x1 block of a 4x4x8 slice. The times are simulated.
32 devices in a mesh: dp: 1 (over z), tp: 32 (over y, x, core).
Axes of the slice: x: 4, y: 4, z: 1, core: 2. Of those that a mesh axis runs over, the one named last changes fastest.
The devices are a block of a 4x4x8 slice.
Arguments:
- x_tokens: bfloat16 [1, 4096, 2048], P('dp', 'tp')
- ln1_gain: float32 [2, 2048], replicated
- ln1_bias: float32 [2, 2048], replicated
- ln2_gain: float32 [2, 2048], replicated
- ln2_bias: float32 [2, 2048], replicated
- w_qkv: bfloat16 [2, 2048, 3, 32, 64], P(None, None, None, 'tp')
- w_out: bfloat16 [2, 32, 64, 2048], P(None, 'tp')
- b_out: float32 [2, 2048], replicated
- w_up: bfloat16 [2, 2048, 8192], P(None, None, 'tp')
- b_up: float32 [2, 8192], P(None, 'tp')
- w_down: bfloat16 [2, 8192, 2048], P(None, 'tp')
- b_down: float32 [2, 2048], replicated
Outputs:
- output: bfloat16 [1, 4096, 2048], P('dp', 'tp')
All inputs are finite; a program needn't handle non-finite values.
Results may differ from a plain program's by a relative error of at most 0.011077.
Values are sent between devices in bfloat16 or wider.
A program may use at most 768 MiB of HBM per device.

v0:
```python
import math
import jax
import jax.numpy as jnp
from jax import lax
from jax.sharding import PartitionSpec as P


def layer_norm(resid, gain, shift):
    row_mean = jnp.mean(resid, axis=-1, keepdims=True)
    centered = resid - row_mean
    variance = jnp.mean(centered * centered, axis=-1, keepdims=True)
    return (centered * lax.rsqrt(variance + 1e-5) * gain + shift).astype(jnp.bfloat16)


def solution(mesh):
    tp_size = mesh.shape["tp"]

    def scatter_rows(partial):
        batch, seq_len, width = partial.shape
        pieces = partial.astype(jnp.bfloat16).reshape(batch, tp_size, seq_len // tp_size, width)
        received = lax.all_to_all(pieces, "tp", 1, 1, tiled=True)
        return jnp.sum(received.astype(jnp.float32), axis=1)

    def local_forward(x_local, ln1_gain, ln1_bias, ln2_gain, ln2_bias, w_qkv, w_out, b_out, w_up, b_up, w_down, b_down):
        seq_len = x_local.shape[1] * tp_size
        scale = 1.0 / math.sqrt(w_out.shape[2])
        positions = jnp.arange(seq_len)
        causal = positions[:, None] >= positions[None, :]
        resid = x_local.astype(jnp.float32)
        for layer in range(w_qkv.shape[0]):
            normed = layer_norm(resid, ln1_gain[layer], ln1_bias[layer])
            gathered = lax.all_gather(normed, "tp", axis=1, tiled=True)
            qkv_proj = jnp.einsum("bsd,dthe->tbhse", gathered, w_qkv[layer], preferred_element_type=jnp.float32).astype(jnp.bfloat16)
            scores = jnp.einsum("bhqe,bhke->bhqk", qkv_proj[0], qkv_proj[1], preferred_element_type=jnp.float32) * scale
            attn_probs = jax.nn.softmax(jnp.where(causal, scores, -1e30), axis=-1).astype(jnp.bfloat16)
            attn_heads = jnp.einsum("bhqk,bhke->bhqe", attn_probs, qkv_proj[2], preferred_element_type=jnp.float32).astype(jnp.bfloat16)
            partial = jnp.einsum("cirf,ife->cre", attn_heads, w_out[layer], preferred_element_type=jnp.float32)
            resid = resid + (scatter_rows(partial) + b_out[layer])
            normed_mlp = layer_norm(resid, ln2_gain[layer], ln2_bias[layer])
            gathered_mlp = lax.all_gather(normed_mlp, "tp", axis=1, tiled=True)
            pre_act = jnp.einsum("bsd,df->bsf", gathered_mlp, w_up[layer], preferred_element_type=jnp.float32) + b_up[layer]
            hidden = jax.nn.gelu(pre_act, approximate=True).astype(jnp.bfloat16)
            partial_mlp = jnp.einsum("bsf,fd->bsd", hidden, w_down[layer], preferred_element_type=jnp.float32)
            resid = resid + (scatter_rows(partial_mlp) + b_down[layer])
        return resid.astype(jnp.bfloat16)

    rows_spec = P("dp", "tp", None)
    in_specs = (rows_spec, P(), P(), P(), P(), P(None, None, None, "tp", None), P(None, "tp", None, None), P(), P(None, None, "tp"), P(None, "tp"), P(None, "tp", None), P())
    return jax.shard_map(local_forward, mesh=mesh, in_specs=in_specs, out_specs=rows_spec, check_vma=False)
```

profile of v0, /device:TPU:97, one launch (start us, length us, event | category | flops | bytes accessed | tf_op | source)
XLA Modules:
  0.0 1430.9 jit_solution(13933298614013752487)
XLA Ops:
  6.6 1.2 convert_reduce_fusion.4
  7.8 1.3 fusion.62
  9.1 1.4 fusion.113
  10.5 1.4 fusion.114
  11.9 2.2 fusion.65
  14.2 2.4 fusion.109
  16.6 69.3 %all-gather.5.cloned.1.call-done = bf16[1,4096,2048]{2,1,0:T(8,128)(2,1)} async-done(((bf16[1,128,2048]{2,1,0:T(8,128)(2,1)}), bf16[1,4096,2048]{2,1,0:T(8,128)(2,1)}) %all-gather.5.cloned.1.call-update) | async-done | bytes 16777232 | tf_op jit(solution)/shard_map/all_gather | solution.py:32
  85.9 9.2 fusion.12
  95.3 24.2 %fusion.2 = (f32[4096]{0:T(1024)S(1)}, f32[4096,4096]{0,1:T(8,128)}) fusion(bf16[3,1,1,4096,64]{3,4,0,1,2:T(8,128)(2,1)S(1)} %convert_bitcast_fusion.1), kind=kOutput, calls=%fused_computation.9 | convolution fusion | flops 2214588416 | bytes 68173824 | tf_op jit(solution)/shard_map/bhqe,bhke->bhqk/dot_general | solution.py:34
  119.5 21.8 %fusion = f32[4096]{0:T(1024)S(1)} fusion(f32[4096,4096]{0,1:T(8,128)} %get-tuple-element.26, f32[4096]{0:T(1024)S(1)} %get-tuple-element.25), kind=kLoop, calls=%fused_computation.7 | loop fusion | flops 83881984 | bytes 67141632 | tf_op jit(solution)/shard_map/reduce_sum | solution.py:35
  141.3 40.0 %convolution_convert_fusion.1 = bf16[4096,2048]{1,0:T(8,128)(2,1)} fusion(f32[4096,4096]{0,1:T(8,128)} %get-tuple-element.26, f32[4096]{0:T(1024)S(1)} %fusion, f32[4096]{0:T(1024)S(1)} %get-tuple-element.25, bf16[3,1,1,4096,64]{3,4,0,1,2:T(8,128)(2,1)S(1)} %convert_bitcast_fusion.1, bf16[2,1,64,2048]{3,2,1,0:T(8,128)(2,1)S(1)} %copy-done.17), kind=kOutput, calls=%fused_computation.26 | convolution fusion | flops 3330539520 | bytes 84705280 | tf_op jit(solution)/shard_map/cirf,ife->cre/dot_general | solution.py:37
  181.3 4.3 all-to-all-start
  187.6 201.6 %all-to-all-done = bf16[1,32,128,2048]{3,2,0,1:T(8,128)(2,1)} async-done(((bf16[1,32,128,2048]{3,2,0,1:T(8,128)(2,1)}), bf16[1,32,128,2048]{3,2,0,1:T(8,128)(2,1)}, u32[]{:S(2)}, u32[]{:S(2)}) %all-to-all-start) | async-done | bytes 16777248 | tf_op jit(solution)/shard_map/all_to_all | solution.py:21
  389.2 7.0 convert_reduce_fusion.3
  396.8 1.1 add_convert_fusion.2
  398.6 86.4 %all-gather.7.cloned.1.call-done = bf16[1,4096,2048]{2,1,0:T(8,128)(2,1)} async-done(((bf16[1,128,2048]{2,1,0:T(8,128)(2,1)}), bf16[1,4096,2048]{2,1,0:T(8,128)(2,1)}) %all-gather.7.cloned.1.call-update) | async-done | bytes 16777232 | tf_op jit(solution)/shard_map/all_gather | solution.py:40
  485.0 24.7 %convolution_convert_fusion.3 = bf16[4096,2048]{1,0:T(8,128)(2,1)} fusion(bf16[1,4096,2048]{2,1,0:T(8,128)(2,1)} %all-gather.7.cloned.1.call-done, f32[256]{0:T(256)S(1)} %bitcast.180, bf16[2,256,2048]{2,1,0:T(8,128)(2,1)} %param.22, bf16[2,2048,256]{2,1,0:T(8,128)(2,1)} %param.20), kind=kOutput, calls=%fused_computation.28 | convolution fusion | flops 8608808960 | bytes 35652608 | tf_op jit(solution)/shard_map/bsf,fd->bsd/dot_general | solution.py:43
  509.7 4.3 all-to-all-start.1
  514.7 202.9 %all-to-all-done.1 = bf16[1,32,128,2048]{3,2,0,1:T(8,128)(2,1)} async-done(((bf16[1,32,128,2048]{3,2,0,1:T(8,128)(2,1)}), bf16[1,32,128,2048]{3,2,0,1:T(8,128)(2,1)}, u32[]{:S(2)}, u32[]{:S(2)}) %all-to-all-start.1) | async-done | bytes 16777248 | tf_op jit(solution)/shard_map/all_to_all | solution.py:21
  717.7 6.9 convert_reduce_fusion.2
  727.1 86.9 %all-gather.9.cloned.1.call-done = bf16[1,4096,2048]{2,1,0:T(8,128)(2,1)} async-done(((bf16[1,128,2048]{2,1,0:T(8,128)(2,1)}), bf16[1,4096,2048]{2,1,0:T(8,128)(2,1)}) %all-gather.9.cloned.1.call-update) | async-done | bytes 16777232 | tf_op jit(solution)/shard_map/all_gather | solution.py:32
  813.9 9.4 fusion.8
  823.5 24.2 %fusion.3 = (f32[4096]{0:T(1024)S(1)}, f32[4096,4096]{0,1:T(8,128)}) fusion(bf16[3,1,1,4096,64]{3,4,0,1,2:T(8,128)(2,1)S(1)} %convert_bitcast_fusion), kind=kOutput, calls=%fused_computation.10 | convolution fusion | flops 2214588416 | bytes 68173824 | tf_op jit(solution)/shard_map/bhqe,bhke->bhqk/dot_general | solution.py:34
  847.7 21.7 %fusion.1 = f32[4096]{0:T(1024)S(1)} fusion(f32[4096,4096]{0,1:T(8,128)} %get-tuple-element.28, f32[4096]{0:T(1024)S(1)} %get-tuple-element.27), kind=kLoop, calls=%fused_computation.8 | loop fusion | flops 83881984 | bytes 67141632 | tf_op jit(solution)/shard_map/reduce_sum | solution.py:35
  869.5 39.7 %convolution_convert_fusion = bf16[4096,2048]{1,0:T(8,128)(2,1)} fusion(f32[4096,4096]{0,1:T(8,128)} %get-tuple-element.28, f32[4096]{0:T(1024)S(1)} %fusion.1, f32[4096]{0:T(1024)S(1)} %get-tuple-element.27, bf16[3,1,1,4096,64]{3,4,0,1,2:T(8,128)(2,1)S(1)} %convert_bitcast_fusion, bf16[2,1,64,2048]{3,2,1,0:T(8,128)(2,1)S(1)} %copy-done.17), kind=kOutput, calls=%fused_computation.25 | convolution fusion | flops 3330539520 | bytes 84705280 | tf_op jit(solution)/shard_map/cirf,ife->cre/dot_general | solution.py:37
  909.2 211.0 %all_to_all.20 = bf16[1,32,128,2048]{3,2,0,1:T(8,128)(2,1)S(1)} all-to-all(bf16[1,32,128,2048]{3,2,0,1:T(8,128)(2,1)} %bitcast.157), channel_id=1, replica_groups=mesh['dp'=1,'tp'=32] {'tp'}, dimensions={1} | all-to-all | bytes 33554432 | tf_op jit(solution)/shard_map/all_to_all | solution.py:21
  1120.2 2.8 convert_reduce_fusion.1
  1123.5 1.0 add_convert_fusion
  1124.6 66.9 %all-gather.11.cloned.1.call-done = bf16[1,4096,2048]{2,1,0:T(8,128)(2,1)} async-done(((bf16[1,128,2048]{2,1,0:T(8,128)(2,1)}), bf16[1,4096,2048]{2,1,0:T(8,128)(2,1)}) %all-gather.11.cloned.1.call-update) | async-done | bytes 16777232 | tf_op jit(solution)/shard_map/all_gather | solution.py:40
  1191.5 24.4 %convolution_convert_fusion.2 = bf16[4096,2048]{1,0:T(8,128)(2,1)} fusion(bf16[1,4096,2048]{2,1,0:T(8,128)(2,1)} %all-gather.11.cloned.1.call-done, f32[256]{0:T(256)S(1)} %bitcast.179, bf16[2,256,2048]{2,1,0:T(8,128)(2,1)S(1)} %copy-done.16, bf16[2,2048,256]{2,1,0:T(8,128)(2,1)} %param.20), kind=kOutput, calls=%fused_computation.27 | convolution fusion | flops 8608808960 | bytes 35652608 | tf_op jit(solution)/shard_map/bsf,fd->bsd/dot_general | solution.py:43
  1215.9 204.2 %all_to_all.21 = bf16[1,32,128,2048]{3,2,0,1:T(8,128)(2,1)S(1)} all-to-all(bf16[1,32,128,2048]{3,2,0,1:T(8,128)(2,1)} %bitcast.158), channel_id=1, replica_groups=mesh['dp'=1,'tp'=32] {'tp'}, dimensions={1} | all-to-all | bytes 33554432 | tf_op jit(solution)/shard_map/all_to_all | solution.py:21
  1420.2 2.8 convert_reduce_fusion
  (67 shorter events, 8.2 us)
Async XLA Ops:
  6.5 79.3 %all-gather.5.cloned.1.call-start = ((), (), s32[]{:S(2)}) async-start(), calls=%async_computation.4 | async-start | bytes 17301504 | tf_op jit(solution)/shard_map/all_gather | solution.py:32
  119.5 21.8 %copy-start.17 = (bf16[2,1,64,2048]{3,2,1,0:T(8,128)(2,1)S(1)}, bf16[2,1,64,2048]{3,2,1,0:T(8,128)(2,1)}, u32[]{:S(2)}) copy-start(bf16[2,1,64,2048]{3,2,1,0:T(8,128)(2,1)} %param.18) | copy-start | bytes 1572868
  181.3 4.4 copy-start.10
  181.3 5.1 copy-start.11
  181.3 5.7 copy-start.12
  181.3 207.9 %all-to-all-start = ((bf16[1,32,128,2048]{3,2,0,1:T(8,128)(2,1)}), bf16[1,32,128,2048]{3,2,0,1:T(8,128)(2,1)}, u32[]{:S(2)}, u32[]{:S(2)}) async-start(bf16[1,32,128,2048]{3,2,0,1:T(8,128)(2,1)} %bitcast.155), calls=%async_computation | async-start | bytes 33554432 | tf_op jit(solution)/shard_map/all_to_all | solution.py:21
  185.6 210.6 %copy-start = (bf16[1,128,2048]{2,1,0:T(8,128)(2,1)S(1)}, bf16[1,128,2048]{2,1,0:T(8,128)(2,1)}, u32[]{:S(2)}) copy-start(bf16[1,128,2048]{2,1,0:T(8,128)(2,1)} %param.12) | copy-start | bytes 1572868
  185.7 212.3 %copy-start.14 = (f32[2,256]{1,0:T(2,128)S(1)}, f32[2,256]{1,0:T(2,128)}, u32[]{:S(2)}) copy-start(f32[2,256]{1,0:T(2,128)} %param.21) | copy-start | bytes 6148
  185.7 299.3 %all-gather.7.cloned.1.call-start = ((), (), s32[]{:S(2)}) async-start(), calls=%async_computation.5 | async-start | bytes 17301504 | tf_op jit(solution)/shard_map/all_gather | solution.py:40
  509.7 4.4 copy-start.13
  509.7 208.0 %all-to-all-start.1 = ((bf16[1,32,128,2048]{3,2,0,1:T(8,128)(2,1)}), bf16[1,32,128,2048]{3,2,0,1:T(8,128)(2,1)}, u32[]{:S(2)}, u32[]{:S(2)}) async-start(bf16[1,32,128,2048]{3,2,0,1:T(8,128)(2,1)} %bitcast.156), calls=%async_computation.1 | async-start | bytes 33554432 | tf_op jit(solution)/shard_map/all_to_all | solution.py:21
  514.0 211.9 %copy-start.6 = (f32[1,2048]{1,0:T(1,128)S(1)}, f32[1,2048]{1,0:T(1,128)}, u32[]{:S(2)}) copy-start(f32[1,2048]{1,0:T(1,128)} %get-tuple-element.17) | copy-start | bytes 24580
  514.0 211.9 %copy-start.7 = (f32[1,2048]{1,0:T(1,128)S(1)}, f32[1,2048]{1,0:T(1,128)}, u32[]{:S(2)}) copy-start(f32[1,2048]{1,0:T(1,128)} %get-tuple-element.19) | copy-start | bytes 24580
  514.0 299.9 %copy-start.3 = (bf16[1,2048,3,1,64]{1,4,2,3,0:T(8,128)(2,1)S(1)}, bf16[1,2048,3,1,64]{1,4,2,3,0:T(8,128)(2,1)}, u32[]{:S(2)}) copy-start(bf16[1,2048,3,1,64]{1,4,2,3,0:T(8,128)(2,1)} %get-tuple-element.9) | copy-start | bytes 2359300
  514.0 299.9 %all-gather.9.cloned.1.call-start = ((), (), s32[]{:S(2)}) async-start(), calls=%async_computation.6 | async-start | bytes 17301504 | tf_op jit(solution)/shard_map/all_gather | solution.py:32
  724.9 1.0 copy-start.1
  727.0 464.5 %all-gather.11.cloned.1.call-start = ((), (), s32[]{:S(2)}) async-start(), calls=%async_computation.7 | async-start | bytes 17301504 | tf_op jit(solution)/shard_map/all_gather | solution.py:40
  1120.1 2.8 copy-start.2
  1120.1 2.8 copy-start.8
  1120.2 3.3 copy-start.4
  1120.2 3.3 copy-start.5
  1120.2 71.4 %copy-start.15 = (f32[1,256]{1,0:T(1,128)S(1)}, f32[1,256]{1,0:T(1,128)}, u32[]{:S(2)}) copy-start(f32[1,256]{1,0:T(1,128)} %get-tuple-element.23) | copy-start | bytes 3076
  1120.2 71.3 %copy-start.16 = (bf16[2,256,2048]{2,1,0:T(8,128)(2,1)S(1)}, bf16[2,256,2048]{2,1,0:T(8,128)(2,1)}, u32[]{:S(2)}) copy-start(bf16[2,256,2048]{2,1,0:T(8,128)(2,1)} %param.22) | copy-start | bytes 6291460
  1420.2 2.8 copy-start.9
Sparse Core Ops, SparseCore 0:
  14.3 71.5 all-gather.4
  398.1 86.8 all-gather.6
  727.1 86.7 all-gather.8
  1124.7 66.7 all-gather.10
where the time goes:
time: 1440 us; the launch traced here: 1430 us
  waiting for transfers between devices  714 us (50%)
  blocking collectives  415 us (29%)
  matrix products  196 us (14%)
  other arithmetic  73.9 us (5%)
    all_to_all x2, blocking collectives, scatter_rows(): received = lax.all_to_all(pieces, 'tp', 1, 1, tiled=True)  415 us
    all_to_all x2, waiting for transfers between devices, scatter_rows(): received = lax.all_to_all(pieces, 'tp', 1, 1, tiled=True)  405 us
    all_gather x2, waiting for transfers between devices, local_forward(): gathered = lax.all_gather(normed, 'tp', axis=1, tiled=True)  156 us
    all_gather x2, waiting for transfers between devices, local_forward(): gathered_mlp = lax.all_gather(normed_mlp, 'tp', axis=1, tiled=True)  153 us
    dot_general x2, matrix products, local_forward(): jnp.einsum('cirf,ife->cre', attn_heads, w_out[layer], preferred_element_t...  79.7 us
    dot_general x2, matrix products, local_forward(): jnp.einsum('bsf,fd->bsd', hidden, w_down[layer], preferred_element_type=j...  49.1 us
    dot_general x2, matrix products, local_forward(): jnp.einsum('bhqe,bhke->bhqk', qkv_proj[0], qkv_proj[1], preferred_element...  48.4 us
    reduce_sum x2, other arithmetic, local_forward(): jax.nn.softmax(jnp.where(causal, scores, -1e+30), axis=-1)  43.5 us
  transfers between devices with their start and end apart: 6, of which 6 were waited for; matrix products, arithmetic and copies ran while one was open for 0% of the time, Pallas kernels for 0%

commit v1 on v0

v1 whole, which is shorter than its diff:
```python
import functools
import math
import jax
import jax.numpy as jnp
from jax import lax
from jax.experimental import pallas as pl
from jax.experimental.pallas import tpu as pltpu
from jax.sharding import PartitionSpec as P

F32 = jnp.float32
BF16 = jnp.bfloat16
CORES = 2
NT = (((1,), (1,)), ((), ()))


def layer_norm(resid, gain, shift):
    row_mean = jnp.mean(resid, axis=-1, keepdims=True)
    centered = resid - row_mean
    variance = jnp.mean(centered * centered, axis=-1, keepdims=True)
    return (centered * lax.rsqrt(variance + 1e-5) * gain + shift).astype(BF16)


def attention_kernel(scale, block, q_ref, k_ref, v_ref, o_ref):
    seq, dim = q_ref.shape
    rows = lax.broadcasted_iota(jnp.int32, (block, block), 0)
    cols = lax.broadcasted_iota(jnp.int32, (block, block), 1)

    def q_step(i, _):
        q = q_ref[pl.ds(pl.multiple_of(i * block, block), block), :]

        def scores(j):
            k = k_ref[pl.ds(pl.multiple_of(j * block, block), block), :]
            return lax.dot_general(q, k, NT, preferred_element_type=F32) * scale

        def update(s, j, carry):
            m, l, acc = carry
            m_new = jnp.maximum(m, jnp.max(s, axis=-1, keepdims=True))
            p = jnp.exp(s - m_new)
            alpha = jnp.exp(m - m_new)
            v = v_ref[pl.ds(pl.multiple_of(j * block, block), block), :]
            acc = acc * alpha + jnp.dot(p.astype(BF16), v, preferred_element_type=F32)
            return m_new, l * alpha + jnp.sum(p, axis=-1, keepdims=True), acc

        def k_step(j, carry):
            return update(scores(j), j, carry)

        init = (jnp.full((block, 1), -1e30, F32), jnp.zeros((block, 1), F32), jnp.zeros((block, dim), F32))
        carry = lax.fori_loop(0, i, k_step, init)
        _, l, acc = update(jnp.where(rows >= cols, scores(i), -1e30), i, carry)
        o_ref[pl.ds(pl.multiple_of(i * block, block), block), :] = (acc / l).astype(BF16)
        return 0

    lax.fori_loop(0, seq // block, q_step, 0)


def attention(q, k, v, scale):
    seq, dim = q.shape
    flops = 2 * seq * seq * dim
    return pl.pallas_call(
        functools.partial(attention_kernel, scale, 512),
        out_shape=jax.ShapeDtypeStruct((seq, dim), BF16),
        in_specs=[pl.BlockSpec(memory_space=pltpu.VMEM)] * 3,
        out_specs=pl.BlockSpec(memory_space=pltpu.VMEM),
        cost_estimate=pl.CostEstimate(flops=flops * 8, bytes_accessed=8 * seq * dim, transcendentals=seq * seq // 2),
        name="attention",
    )(q, k, v)


def solution(mesh):
    tp = mesh.shape["tp"]
    side = math.isqrt(tp // CORES)
    row_groups = [[(y * side + x) * CORES + c for x in range(side)] for y in range(side) for c in range(CORES)]
    col_groups = [[(y * side + x) * CORES + c for y in range(side) for c in range(CORES)] for x in range(side)]
    col = side * CORES

    def local_forward(x_local, ln1_gain, ln1_bias, ln2_gain, ln2_bias, w_qkv, w_out, b_out, w_up, b_up, w_down, b_down):
        _, share, width = x_local.shape
        layers, _, three, _, dim = w_qkv.shape
        scale = 1.0 / math.sqrt(dim)
        hidden = w_up.shape[2]
        wq_t = jnp.transpose(w_qkv, (0, 2, 3, 4, 1)).reshape(layers, three * dim, width)
        bup_all = lax.all_gather(b_up, "tp", axis=0, axis_index_groups=col_groups)
        gathered = []
        for layer in range(layers):
            gathered.append((
                lax.all_gather(wq_t[layer], "tp", axis=0, axis_index_groups=col_groups),
                lax.all_gather(w_out[layer].reshape(dim, width), "tp", axis=0),
                lax.all_gather(w_up[layer], "tp", axis=0, axis_index_groups=col_groups),
                lax.all_gather(w_down[layer], "tp", axis=0, axis_index_groups=col_groups),
            ))
        resid = x_local[0].astype(F32)
        for layer in range(layers):
            gq, go, gu, gd = gathered[layer]
            normed = layer_norm(resid, ln1_gain[layer], ln1_bias[layer])
            rows = lax.all_gather(normed, "tp", axis=0, axis_index_groups=row_groups, tiled=True)
            qkv = jnp.einsum("sd,ged->gse", rows, gq, preferred_element_type=F32).astype(BF16)
            qkv = lax.all_to_all(qkv, "tp", 0, 0, axis_index_groups=col_groups, tiled=True)
            qkv = qkv.reshape(side, CORES, side, share, three * dim).transpose(0, 2, 1, 3, 4).reshape(tp * share, three, dim)
            o = attention(qkv[:, 0], qkv[:, 1], qkv[:, 2], scale)
            o = lax.all_to_all(o.reshape(tp, share, dim), "tp", 0, 0, tiled=True)
            o = o.transpose(1, 0, 2).reshape(share, tp * dim)
            attn = jnp.dot(o, go.reshape(tp * dim, width), preferred_element_type=F32)
            resid = resid + (attn + b_out[layer])
            normed = layer_norm(resid, ln2_gain[layer], ln2_bias[layer])
            rows = lax.all_gather(normed, "tp", axis=0, axis_index_groups=row_groups, tiled=True)
            pre = jnp.einsum("sd,gdf->sgf", rows, gu, preferred_element_type=F32) + bup_all[:, layer]
            act = jax.nn.gelu(pre, approximate=True).astype(BF16)
            z = jnp.einsum("sgf,gfd->sd", act, gd, preferred_element_type=F32).astype(BF16)
            z = lax.all_to_all(z.reshape(side, share, width), "tp", 0, 0, axis_index_groups=row_groups, tiled=True)
            resid = resid + (jnp.sum(z.astype(F32), axis=0) + b_down[layer])
        return resid.astype(BF16)[None]

    rows_spec = P("dp", "tp", None)
    in_specs = (rows_spec, P(), P(), P(), P(), P(None, None, None, "tp", None), P(None, "tp", None, None), P(), P(None, None, "tp"), P(None, "tp"), P(None, "tp", None), P())
    return jax.shard_map(local_forward, mesh=mesh, in_specs=in_specs, out_specs=rows_spec, check_vma=False)
```

time: 1440 us -> 599 us (0.42)
  waiting for transfers between devices: 714 us -> 312 us
  blocking collectives: 415 us -> 73.6 us
  matrix products: 196 us -> 58 us
  other arithmetic: 73.9 us -> 12.4 us
  Pallas kernels: 0 us -> 56.3 us
  local copies, waits for them, and re-layouts: 9.05 us -> 42.5 us
    all_to_all x2, blocking collectives: 415 us -> 57.3 us  [the longest x1 28.9 us: local_forward(): lax.all_to_all(z.reshape(side, share, width), 'tp', 0, 0, axis_index_grou...]
    all_to_all x2 -> x4, waiting for transfers between devices: 405 us -> 70.3 us  [the longest x1 25.2 us: local_forward(): lax.all_to_all(z.reshape(side, share, width), 'tp', 0, 0, axis_index_grou...]
    dot_general x6, matrix products: 177 us -> 58 us  [the longest x2 33.5 us: local_forward(): jnp.einsum('sgf,gfd->sd', act, gd, preferred_element_type=F32).astype(BF16)]
    all_gather x4 -> x12, waiting for transfers between devices: 309 us -> 239 us  [the longest x4 107 us: local_forward(): lax.all_gather(normed, 'tp', axis=0, axis_index_groups=row_groups, tiled=...]
    reduce_sum x6 -> x2, other arithmetic: 63 us -> 2.48 us  [local_forward(): resid = resid + (jnp.sum(z.astype(F32), axis=0) + b_down[layer])]
    pallas_call x0 -> x2, Pallas kernels: none -> 56.3 us  [attention(): pl.pallas_call(functools.partial(attention_kernel, scale, 512), out_shape...]
    reshape x0 -> x8, local copies, waits for them, and re-layouts: none -> 21.3 us  [the longest x6 16.6 us: local_forward(): qkv.reshape(side, CORES, side, share, three * dim).transpose(0, 2, 1, 3, 4)]
    unnamed x2 -> x0, matrix products: 18.6 us -> none
  transfers between devices with their start and end apart: 6 -> 16, of which waited for: 6 -> 12; matrix products, arithmetic and copies ran while one was open for 0% -> 15% of each run, Pallas kernels for 0% -> 10%
where the time goes in v1:
time: 599 us; the launch traced here: 590 us
  waiting for transfers between devices  312 us (52%)
  blocking collectives  73.6 us (12%)
  matrix products  58 us (10%)
  Pallas kernels  56.3 us (9%)
  local copies, waits for them, and re-layouts  42.5 us (7%)
  starting transfers between devices  20.4 us (3%)
  between operations  14.3 us (2%)
  other arithmetic  12.4 us (2%)
    all_gather x4, waiting for transfers between devices, local_forward(): lax.all_gather(normed, 'tp', axis=0, axis_index_groups=row_groups, tiled=...  107 us
    all_gather x2, waiting for transfers between devices, local_forward(): lax.all_gather(w_down[layer], 'tp', axis=0, axis_index_groups=col_groups)  87.5 us
    pallas_call x2, Pallas kernels, attention(): pl.pallas_call(functools.partial(attention_kernel, scale, 512), out_shape...  56.3 us
    all_gather x2, waiting for transfers between devices, local_forward(): lax.all_gather(wq_t[layer], 'tp', axis=0, axis_index_groups=col_groups)  40.4 us
    dot_general x2, matrix products, local_forward(): jnp.einsum('sgf,gfd->sd', act, gd, preferred_element_type=F32).astype(BF16)  33.5 us
    all_to_all x1, blocking collectives, local_forward(): lax.all_to_all(z.reshape(side, share, width), 'tp', 0, 0, axis_index_grou...  28.9 us
    all_to_all x1, blocking collectives, local_forward(): lax.all_to_all(qkv, 'tp', 0, 0, axis_index_groups=col_groups, tiled=True)  28.4 us
    all_to_all x1, waiting for transfers between devices, local_forward(): lax.all_to_all(z.reshape(side, share, width), 'tp', 0, 0, axis_index_grou...  25.2 us
  transfers between devices with their start and end apart: 16, of which 12 were waited for; matrix products, arithmetic and copies ran while one was open for 15% of the time, Pallas kernels for 10%

profile of v1, /device:TPU:97, one launch (start us, length us, event | category | flops | bytes accessed | tf_op | source)
XLA Modules:
  0.0 589.6 jit_solution(9127011367941214731)
XLA Ops:
  18.7 3.1 fusion.90
  21.8 23.1 %all-gather.17.cloned.1.call-done = bf16[512,2048]{1,0:T(8,128)(2,1)} async-done(((bf16[128,2048]{1,0:T(8,128)(2,1)}), bf16[512,2048]{1,0:T(8,128)(2,1)}) %all-gather.17.cloned.1.call-update) | async-done | bytes 2097168 | tf_op jit(solution)/shard_map/all_gather | solution.py:95
  44.9 40.4 %all-gather.19.cloned.1.call-done = bf16[8,192,2048]{2,1,0:T(8,128)(2,1)} async-done(((bf16[1,192,2048]{2,1,0:T(8,128)(2,1)}), bf16[8,192,2048]{2,1,0:T(8,128)(2,1)}) %all-gather.19.cloned.1.call-update) | async-done | bytes 6291472 | tf_op jit(solution)/shard_map/all_gather | solution.py:86
  85.3 8.1 %fusion.67 = bf16[8,512,192]{1,2,0:T(8,128)(2,1)} fusion(bf16[8,192,2048]{2,1,0:T(8,128)(2,1)} %all-gather.19.cloned.1.call-done, bf16[512,2048]{1,0:T(8,128)(2,1)} %all-gather.17.cloned.1.call-done), kind=kOutput, calls=%fused_computation.55 | convolution fusion | flops 3222011904 | bytes 9961472 | tf_op jit(solution)/shard_map/sd,ged->gse/dot_general | solution.py:96
  93.4 3.8 all-to-all-start
  97.2 23.7 %all-to-all-done = bf16[8,512,192]{1,2,0:T(8,128)(2,1)S(1)} async-done(((bf16[8,512,192]{1,2,0:T(8,128)(2,1)}), bf16[8,512,192]{1,2,0:T(8,128)(2,1)S(1)}, u32[]{:S(2)}, u32[]{:S(2)}) %all-to-all-start) | async-done | bytes 1572896 | tf_op jit(solution)/shard_map/all_to_all | solution.py:97
  121.3 3.6 copy.52
  124.9 2.9 reshape.83
  131.9 28.2 %attention.2 = bf16[4096,64]{1,0:T(8,128)(2,1)} custom-call(bf16[4096,64]{1,0:T(8,128)(2,1)} %bitcast.169, bf16[4096,64]{1,0:T(8,128)(2,1)} %bitcast.171, bf16[4096,64]{1,0:T(8,128)(2,1)} %bitcast.167), custom_call_target="tpu_custom_call" | custom-call | flops 17179869184 | bytes 2097152 | tf_op jit(solution)/shard_map/attention/pallas_call | solution.py:59
  162.4 5.9 %all-to-all-start.1 = ((bf16[32,128,64]{1,2,0:T(8,128)(2,1)}), bf16[32,128,64]{1,2,0:T(8,128)(2,1)S(1)}, u32[]{:S(2)}, u32[]{:S(2)}) async-start(bf16[32,128,64]{1,2,0:T(8,128)(2,1)} %copy.33), calls=%async_computation.1 | async-start | bytes 1048576 | tf_op jit(solution)/shard_map/all_to_all | solution.py:100
  168.7 10.7 %all-to-all-done.1 = bf16[32,128,64]{1,2,0:T(8,128)(2,1)S(1)} async-done(((bf16[32,128,64]{1,2,0:T(8,128)(2,1)}), bf16[32,128,64]{1,2,0:T(8,128)(2,1)S(1)}, u32[]{:S(2)}, u32[]{:S(2)}) %all-to-all-start.1) | async-done | bytes 524320 | tf_op jit(solution)/shard_map/all_to_all | solution.py:100
  179.4 4.8 fusion.102
  186.4 16.3 %all-gather.3 = f32[8,2,256]{2,1,0:T(2,128)S(1)} all-gather(f32[1,2,256]{2,1,0:T(2,128)S(1)} %bitcast.189), channel_id=3, replica_groups={{0,1,8,9,16,17,24,25},{2,3,10,11,18,19,26,27},{4,5,12,13,20,21,28,29},{..., dimensions={0}, use_global_device_ids=true | all-gather | bytes 18432 | tf_op jit(solution)/shard_map/all_gather | solution.py:82
  202.8 38.7 %all-gather.25.cloned.1.call-done = bf16[8,256,2048]{2,1,0:T(8,128)(2,1)} async-done(((bf16[1,256,2048]{2,1,0:T(8,128)(2,1)}), bf16[8,256,2048]{2,1,0:T(8,128)(2,1)}) %all-gather.25.cloned.1.call-update) | async-done | bytes 8388624 | tf_op jit(solution)/shard_map/all_gather | solution.py:89
  241.4 29.0 %all-gather.21.cloned.1.call-done = bf16[512,2048]{1,0:T(8,128)(2,1)} async-done(((bf16[128,2048]{1,0:T(8,128)(2,1)}), bf16[512,2048]{1,0:T(8,128)(2,1)}) %all-gather.21.cloned.1.call-update) | async-done | bytes 2097168 | tf_op jit(solution)/shard_map/all_gather | solution.py:105
  270.4 16.8 %bitcast_convert_fusion.1 = bf16[512,2048]{1,0:T(8,128)(2,1)} fusion(bf16[8,256,2048]{2,1,0:T(8,128)(2,1)} %all-gather.25.cloned.1.call-done, f32[8,256]{1,0:T(8,128)S(1)} %bitcast.187, bf16[8,2048,256]{2,1,0:T(8,128)(2,1)} %all-gather.23.cloned.1.call-done, bf16[512,2048]{1,0:T(8,128)(2,1)} %all-gather.21.cloned.1.call-done), kind=kOutput, calls=%fused_computation.23 | convolution fusion | flops 8601468928 | bytes 20979712 | tf_op jit(solution)/shard_map/sgf,gfd->sd/dot_general | solution.py:108
  287.2 4.7 all-to-all-start.2
  291.9 25.2 %all-to-all-done.2 = bf16[4,128,2048]{2,1,0:T(8,128)(2,1)} async-done(((bf16[4,128,2048]{2,1,0:T(8,128)(2,1)}), bf16[4,128,2048]{2,1,0:T(8,128)(2,1)}, u32[]{:S(2)}, u32[]{:S(2)}) %all-to-all-start.2) | async-done | bytes 2097184 | tf_op jit(solution)/shard_map/all_to_all | solution.py:109
  323.1 26.2 %all-gather.27.cloned.1.call-done = bf16[512,2048]{1,0:T(8,128)(2,1)} async-done(((bf16[128,2048]{1,0:T(8,128)(2,1)}), bf16[512,2048]{1,0:T(8,128)(2,1)}) %all-gather.27.cloned.1.call-update) | async-done | bytes 2097168 | tf_op jit(solution)/shard_map/all_gather | solution.py:95
  349.4 6.9 %fusion.64 = bf16[8,512,192]{1,2,0:T(8,128)(2,1)S(1)} fusion(bf16[8,192,2048]{2,1,0:T(8,128)(2,1)} %all-gather.29.cloned.1.call-done, bf16[512,2048]{1,0:T(8,128)(2,1)} %all-gather.27.cloned.1.call-done), kind=kOutput, calls=%fused_computation.54 | convolution fusion | flops 3222011904 | bytes 9961472 | tf_op jit(solution)/shard_map/sd,ged->gse/dot_general | solution.py:96
  356.3 28.4 %all_to_all.30 = bf16[8,512,192]{1,2,0:T(8,128)(2,1)S(1)} all-to-all(bf16[8,512,192]{1,2,0:T(8,128)(2,1)S(1)} %fusion.64), channel_id=1, replica_groups={{0,1,8,9,16,17,24,25},{2,3,10,11,18,19,26,27},{4,5,12,13,20,21,28,29},{..., dimensions={0} | all-to-all | bytes 3145728 | tf_op jit(solution)/shard_map/all_to_all | solution.py:97
  386.6 5.0 copy.51
  391.5 2.9 reshape.87
  401.6 28.1 %attention.3 = bf16[4096,64]{1,0:T(8,128)(2,1)} custom-call(bf16[4096,64]{1,0:T(8,128)(2,1)} %bitcast.168, bf16[4096,64]{1,0:T(8,128)(2,1)} %bitcast.170, bf16[4096,64]{1,0:T(8,128)(2,1)} %bitcast.173), custom_call_target="tpu_custom_call" | custom-call | flops 17179869184 | bytes 2097152 | tf_op jit(solution)/shard_map/attention/pallas_call | solution.py:59
  432.0 4.7 all-to-all-start.4
  437.1 10.7 %all-to-all-done.4 = bf16[32,128,64]{1,2,0:T(8,128)(2,1)S(1)} async-done(((bf16[32,128,64]{1,2,0:T(8,128)(2,1)}), bf16[32,128,64]{1,2,0:T(8,128)(2,1)S(1)}, u32[]{:S(2)}, u32[]{:S(2)}) %all-to-all-start.4) | async-done | bytes 524320 | tf_op jit(solution)/shard_map/all_to_all | solution.py:100
  447.8 4.7 fusion.103
  453.9 3.6 all-gather.33.cloned.1.call-done
  457.5 48.9 %all-gather.35.cloned.1.call-done = bf16[8,256,2048]{2,1,0:T(8,128)(2,1)} async-done(((bf16[1,256,2048]{2,1,0:T(8,128)(2,1)}), bf16[8,256,2048]{2,1,0:T(8,128)(2,1)}) %all-gather.35.cloned.1.call-update) | async-done | bytes 8388624 | tf_op jit(solution)/shard_map/all_gather | solution.py:89
  506.4 29.0 %all-gather.31.cloned.1.call-done = bf16[512,2048]{1,0:T(8,128)(2,1)} async-done(((bf16[128,2048]{1,0:T(8,128)(2,1)}), bf16[512,2048]{1,0:T(8,128)(2,1)}) %all-gather.31.cloned.1.call-update) | async-done | bytes 2097168 | tf_op jit(solution)/shard_map/all_gather | solution.py:105
  535.3 16.8 %bitcast_convert_fusion = bf16[512,2048]{1,0:T(8,128)(2,1)} fusion(bf16[8,256,2048]{2,1,0:T(8,128)(2,1)} %all-gather.35.cloned.1.call-done, f32[8,256]{1,0:T(8,128)S(1)} %bitcast.188, bf16[8,2048,256]{2,1,0:T(8,128)(2,1)} %all-gather.33.cloned.1.call-done, bf16[512,2048]{1,0:T(8,128)(2,1)} %all-gather.31.cloned.1.call-done), kind=kOutput, calls=%fused_computation.22 | convolution fusion | flops 8601468928 | bytes 20979712 | tf_op jit(solution)/shard_map/sgf,gfd->sd/dot_general | solution.py:108
  552.1 28.9 %all_to_all.31 = bf16[4,128,2048]{2,1,0:T(8,128)(2,1)S(1)} all-to-all(bf16[4,128,2048]{2,1,0:T(8,128)(2,1)} %bitcast.165), channel_id=1, replica_groups={{0,2,4,6},{1,3,5,7},{8,10,12,14},{9,11,13,15},{16,18,20,22},{17,19,21,2..., dimensions={0} | all-to-all | bytes 4194304 | tf_op jit(solution)/shard_map/all_to_all | solution.py:109
  (89 shorter events, 41.9 us)
Async XLA Ops:
  6.5 9.6 %copy-start.2 = (bf16[2,1,64,2048]{3,2,1,0:T(8,128)(2,1)S(1)}, bf16[2,1,64,2048]{3,2,1,0:T(8,128)(2,1)}, u32[]{:S(2)}) copy-start(bf16[2,1,64,2048]{3,2,1,0:T(8,128)(2,1)} %param.18) | copy-start | bytes 1572868
  6.5 10.5 %copy-start.1 = (bf16[2,2048,256]{2,1,0:T(8,128)(2,1)S(1)}, bf16[2,2048,256]{2,1,0:T(8,128)(2,1)}, u32[]{:S(2)}) copy-start(bf16[2,2048,256]{2,1,0:T(8,128)(2,1)} %param.20) | copy-start | bytes 6291460
  6.6 38.4 %all-gather.17.cloned.1.call-start = ((), (), s32[]{:S(2)}) async-start(), calls=%async_computation.6 | async-start | bytes 2621440 | tf_op jit(solution)/shard_map/all_gather | solution.py:95
  13.1 72.2 %all-gather.19.cloned.1.call-start = ((), (), s32[]{:S(2)}) async-start(), calls=%async_computation.7 | async-start | bytes 7077888 | tf_op jit(solution)/shard_map/all_gather | solution.py:86
  16.0 163.4 %all-gather.37.cloned.1.call-start = ((), (), s32[]{:S(2)}) async-start(), calls=%async_computation.16 | async-start | bytes 8650752 | tf_op jit(solution)/shard_map/all_gather | solution.py:87
  17.0 185.7 %all-gather.23.cloned.1.call-start = ((), (), s32[]{:S(2)}) async-start(), calls=%async_computation.9 | async-start | bytes 9437184 | tf_op jit(solution)/shard_map/all_gather | solution.py:88
  18.6 222.8 %all-gather.25.cloned.1.call-start = ((), (), s32[]{:S(2)}) async-start(), calls=%async_computation.10 | async-start | bytes 9437184 | tf_op jit(solution)/shard_map/all_gather | solution.py:89
  21.8 75.3 %copy-start.3 = (f32[2,2048]{1,0:T(2,128)S(1)}, f32[2,2048]{1,0:T(2,128)}, u32[]{:S(2)}) copy-start(f32[2,2048]{1,0:T(2,128)} %param.19) | copy-start | bytes 49156
  93.4 27.5 %all-to-all-start = ((bf16[8,512,192]{1,2,0:T(8,128)(2,1)}), bf16[8,512,192]{1,2,0:T(8,128)(2,1)S(1)}, u32[]{:S(2)}, u32[]{:S(2)}) async-start(bf16[8,512,192]{1,2,0:T(8,128)(2,1)} %fusion.67), calls=%async_computation | async-start | bytes 3145728 | tf_op jit(solution)/shard_map/all_to_all | solution.py:97
  131.9 36.7 %copy-start.4 = (f32[2,2048]{1,0:T(2,128)S(1)}, f32[2,2048]{1,0:T(2,128)}, u32[]{:S(2)}) copy-start(f32[2,2048]{1,0:T(2,128)} %param.15) | copy-start | bytes 49156
  131.9 36.8 %copy-start.5 = (f32[2,2048]{1,0:T(2,128)S(1)}, f32[2,2048]{1,0:T(2,128)}, u32[]{:S(2)}) copy-start(f32[2,2048]{1,0:T(2,128)} %param.16) | copy-start | bytes 49156
  131.9 47.5 %copy-start = (bf16[1,128,2048]{2,1,0:T(8,128)(2,1)S(1)}, bf16[1,128,2048]{2,1,0:T(8,128)(2,1)}, u32[]{:S(2)}) copy-start(bf16[1,128,2048]{2,1,0:T(8,128)(2,1)} %param.12) | copy-start | bytes 1572868
  162.4 17.0 %all-to-all-start.1 = ((bf16[32,128,64]{1,2,0:T(8,128)(2,1)}), bf16[32,128,64]{1,2,0:T(8,128)(2,1)S(1)}, u32[]{:S(2)}, u32[]{:S(2)}) async-start(bf16[32,128,64]{1,2,0:T(8,128)(2,1)} %copy.33), calls=%async_computation.1 | async-start | bytes 1048576 | tf_op jit(solution)/shard_map/all_to_all | solution.py:100
  168.4 102.0 %all-gather.21.cloned.1.call-start = ((), (), s32[]{:S(2)}) async-start(), calls=%async_computation.8 | async-start | bytes 2621440 | tf_op jit(solution)/shard_map/all_gather | solution.py:105
  179.4 7.0 %copy-start.7 = (f32[2,256]{1,0:T(2,128)S(1)}, f32[2,256]{1,0:T(2,128)}, u32[]{:S(2)}) copy-start(f32[2,256]{1,0:T(2,128)} %param.21) | copy-start | bytes 6148
  185.6 137.6 %all-gather.29.cloned.1.call-start = ((), (), s32[]{:S(2)}) async-start(), calls=%async_computation.12 | async-start | bytes 7077888 | tf_op jit(solution)/shard_map/all_gather | solution.py:86
  287.2 4.8 copy-start.6
  287.2 30.0 %all-to-all-start.2 = ((bf16[4,128,2048]{2,1,0:T(8,128)(2,1)}), bf16[4,128,2048]{2,1,0:T(8,128)(2,1)}, u32[]{:S(2)}, u32[]{:S(2)}) async-start(bf16[4,128,2048]{2,1,0:T(8,128)(2,1)} %bitcast.164), calls=%async_computation.2 | async-start | bytes 4194304 | tf_op jit(solution)/shard_map/all_to_all | solution.py:109
  291.8 57.5 %all-gather.27.cloned.1.call-start = ((), (), s32[]{:S(2)}) async-start(), calls=%async_computation.11 | async-start | bytes 2621440 | tf_op jit(solution)/shard_map/all_gather | solution.py:95
  320.9 116.2 %all-gather.39.cloned.1.call-start = ((), (), s32[]{:S(2)}) async-start(), calls=%async_computation.17 | async-start | bytes 8650752 | tf_op jit(solution)/shard_map/all_gather | solution.py:87
  321.7 135.8 %all-gather.33.cloned.1.call-start = ((), (), s32[]{:S(2)}) async-start(), calls=%async_computation.14 | async-start | bytes 9437184 | tf_op jit(solution)/shard_map/all_gather | solution.py:88
  322.3 184.0 %all-gather.35.cloned.1.call-start = ((), (), s32[]{:S(2)}) async-start(), calls=%async_computation.15 | async-start | bytes 9437184 | tf_op jit(solution)/shard_map/all_gather | solution.py:89
  432.0 15.8 %all-to-all-start.4 = ((bf16[32,128,64]{1,2,0:T(8,128)(2,1)}), bf16[32,128,64]{1,2,0:T(8,128)(2,1)S(1)}, u32[]{:S(2)}, u32[]{:S(2)}) async-start(bf16[32,128,64]{1,2,0:T(8,128)(2,1)} %copy.38), calls=%async_computation.4 | async-start | bytes 1048576 | tf_op jit(solution)/shard_map/all_to_all | solution.py:100
  436.8 98.6 %all-gather.31.cloned.1.call-start = ((), (), s32[]{:S(2)}) async-start(), calls=%async_computation.13 | async-start | bytes 2621440 | tf_op jit(solution)/shard_map/all_gather | solution.py:105
Sparse Core Ops, SparseCore 0:
  13.2 31.6 all-gather.16
  46.5 38.7 all-gather.18
  87.4 52.2 all-gather.36
  141.2 51.4 all-gather.22
  194.2 47.2 all-gather.24
  242.8 27.5 all-gather.20
  272.0 38.7 all-gather.28
  321.0 28.3 all-gather.26
  351.5 52.7 all-gather.38
  405.7 51.7 all-gather.32
  459.1 47.1 all-gather.34
  507.8 27.5 all-gather.30

commit v2 on v1

v2 whole, which is shorter than its diff:
```python
import functools
import math
import jax
import jax.numpy as jnp
from jax import lax
from jax.experimental import pallas as pl
from jax.experimental.pallas import tpu as pltpu
from jax.sharding import PartitionSpec as P

F32 = jnp.float32
BF16 = jnp.bfloat16
CORES = 2
NN = (((1,), (0,)), ((), ()))
NT = (((1,), (1,)), ((), ()))
TN = (((0,), (0,)), ((), ()))
MESH = pl.DeviceIdType.MESH
VMEM = pl.BlockSpec(memory_space=pltpu.VMEM)
HBM = pl.BlockSpec(memory_space=pl.ANY)
DMA = pltpu.SemaphoreType.DMA


def place(side):
    me = lax.axis_index("tp")
    return me, me // (side * CORES), (me // CORES) % side, me % CORES


def index_of(side, y, x, c):
    return (y * side + x) * CORES + c


def dev(index):
    return {"tp": index}


def remote(src, dst, send_sem, recv_sem, index):
    return pltpu.make_async_remote_copy(src_ref=src, dst_ref=dst, send_sem=send_sem, recv_sem=recv_sem, device_id=dev(index), device_id_type=MESH)


def enter(indices):
    barrier = pltpu.get_barrier_semaphore()
    for index in indices:
        pl.semaphore_signal(barrier, inc=1, device_id=dev(index), device_id_type=MESH)
    pl.semaphore_wait(barrier, len(indices))


def norm(resid, gain, shift):
    row_mean = jnp.mean(resid, axis=-1, keepdims=True)
    centered = resid - row_mean
    variance = jnp.mean(centered * centered, axis=-1, keepdims=True)
    return (centered * lax.rsqrt(variance + 1e-5) * gain + shift).astype(BF16)


def ring_order(side):
    return sorted(range(1, side), key=lambda off: min(off, side - off))


def qkv_kernel(side, r_ref, gain_ref, shift_ref, w_hbm, out_ref, w_ref, hbuf, sbuf, w_sem, h_send, h_recv, q_send, q_recv):
    me, y, x, c = place(side)
    col = side * CORES
    mine = y * CORES + c
    offs = ring_order(side)

    def in_col(m):
        return index_of(side, m // CORES, x, m % CORES)

    load = pltpu.make_async_copy(w_hbm, w_ref, w_sem)
    load.start()
    row_peers = [index_of(side, y, (x + off) % side, c) for off in offs]
    enter(row_peers + [in_col((mine + d) % col) for d in range(1, col)])
    hbuf[x] = norm(r_ref[...].astype(F32), gain_ref[...], shift_ref[...])
    sends = [remote(hbuf.at[x], hbuf.at[x], h_send.at[n], h_recv.at[n], row_peers[n]) for n in range(len(offs))]
    for copy in sends:
        copy.start()
    load.wait()

    def slot_copy(k, d, xk):
        return remote(sbuf.at[k, d], out_ref.at[index_of(side, y, xk, c)], q_send.at[k, d], q_recv.at[k, d], in_col((mine + d) % col))

    for k in range(side):
        xk = (x - ([0] + offs)[k] + side) % side
        if k:
            remote(hbuf.at[xk], hbuf.at[xk], h_send.at[k - 1], h_recv.at[k - 1], row_peers[k - 1]).wait_recv()

        def step(n, _):
            d = (n + 1) % col
            g = (mine + d) % col
            part = lax.dot_general(w_ref[g], hbuf[xk], NT, preferred_element_type=F32).astype(BF16)

            @pl.when(d != 0)
            def _():
                sbuf[k, d] = part
                slot_copy(k, d, xk).start()

            @pl.when(d == 0)
            def _():
                out_ref[index_of(side, y, xk, c)] = part

            return 0

        lax.fori_loop(0, col, step, 0)
    for copy in sends:
        copy.wait_send()
    for k in range(side):
        for d in range(1, col):
            slot_copy(k, d, x).wait()


def attention_kernel(side, scale, block, qkv_ref, o_ref, sbuf, send_sem, recv_sem):
    tp, three_dim, share = qkv_ref.shape
    dim = three_dim // 3
    me, _, _, _ = place(side)
    per = block // share
    c2 = scale * math.log2(math.e)
    rows = lax.broadcasted_iota(jnp.int32, (block, block), 0)
    cols = lax.broadcasted_iota(jnp.int32, (block, block), 1)
    enter([(me + d) % tp for d in range(1, tp)])

    def part(i, which):
        return jnp.concatenate([qkv_ref[i * per + n, which * dim : (which + 1) * dim, :] for n in range(per)], axis=1)

    def o_copy(d):
        return remote(sbuf.at[d], o_ref.at[me], send_sem.at[d], recv_sem.at[d], (me + d) % tp)

    def q_step(i, _):
        q = part(i, 0).T

        def scores(j):
            return lax.dot_general(q, part(j, 1), NN, preferred_element_type=F32)

        def update(s, j, carry):
            m, l, acc = carry
            m_new = jnp.maximum(m, jnp.max(s, axis=-1, keepdims=True))
            p = jnp.exp2(s * c2 - m_new * c2)
            alpha = jnp.exp2((m - m_new) * c2)
            acc = acc * alpha + lax.dot_general(p.astype(BF16), part(j, 2), NT, preferred_element_type=F32)
            return m_new, l * alpha + jnp.sum(p, axis=-1, keepdims=True), acc

        init = (jnp.full((block, 1), -1e30, F32), jnp.zeros((block, 1), F32), jnp.zeros((block, dim), F32))
        carry = lax.fori_loop(0, i, lambda j, carry: update(scores(j), j, carry), init)
        _, l, acc = update(jnp.where(rows >= cols, scores(i), -1e30), i, carry)
        o_t = (acc / l).T.astype(BF16)
        for n in range(per):
            d = (i * per + n - me + tp) % tp
            piece = o_t[:, n * share : (n + 1) * share]

            @pl.when(d != 0)
            def _():
                sbuf[d] = piece
                o_copy(d).start()

            @pl.when(d == 0)
            def _():
                o_ref[me] = piece

        return 0

    lax.fori_loop(0, tp * share // block, q_step, 0)

    def drain(d, _):
        o_copy(d).wait()
        return 0

    lax.fori_loop(1, tp, drain, 0)


def mlp_kernel(side, r_ref, o_ref, bo_ref, gain_ref, shift_ref, bu_ref, bd_ref, wo_hbm, wu_hbm, wd_hbm, out_ref,
               wo, wu, wd, hbuf, ubuf, zsend, zrecv, resid, w_sem, h_send, h_recv, z_send, z_recv):
    me, y, x, c = place(side)
    offs = ring_order(side)
    width = r_ref.shape[1]
    share = r_ref.shape[0]
    tile = 256
    loads = [pltpu.make_async_copy(src, dst, w_sem.at[n]) for n, (src, dst) in enumerate(((wo_hbm, wo), (wu_hbm, wu), (wd_hbm, wd)))]
    for load in loads:
        load.start()
    fwd = [index_of(side, y, (x + off) % side, c) for off in offs]
    enter(fwd)
    o_t = o_ref[...].reshape(wo.shape[0], share)
    loads[0].wait()

    def out_step(n, _):
        cs = pl.ds(pl.multiple_of(n * tile, tile), tile)
        resid[:, cs] = r_ref[:, cs].astype(F32) + (lax.dot_general(o_t, wo[:, cs], TN, preferred_element_type=F32) + bo_ref[:, cs])
        return 0

    lax.fori_loop(0, width // tile, out_step, 0)
    hbuf[x] = norm(resid[...], gain_ref[...], shift_ref[...])
    sends = [remote(hbuf.at[x], hbuf.at[x], h_send.at[n], h_recv.at[n], fwd[n]) for n in range(len(offs))]
    for copy in sends:
        copy.start()
    loads[1].wait()
    loads[2].wait()
    back = [index_of(side, y, (x - off + side) % side, c) for off in offs]
    z_copies = [remote(zsend.at[n], zrecv.at[n], z_send.at[n], z_recv.at[n], back[n]) for n in range(len(offs))]
    for k in range(side):
        xk = (x - ([0] + offs)[k] + side) % side
        if k:
            sends[k - 1].wait_recv()

        def up_step(g, _):
            pre = lax.dot_general(hbuf[xk], wu[g], NN, preferred_element_type=F32) + bu_ref[g]
            ubuf[:, pl.ds(pl.multiple_of(g * wu.shape[2], 128), wu.shape[2])] = jax.nn.gelu(pre, approximate=True).astype(BF16)
            return 0

        lax.fori_loop(0, wu.shape[0], up_step, 0)

        def down_step(n, _):
            cs = pl.ds(pl.multiple_of(n * tile, tile), tile)
            z = lax.dot_general(ubuf[...], wd[:, cs], NN, preferred_element_type=F32)
            if k:
                zsend[k - 1, :, cs] = z.astype(BF16)
            else:
                resid[:, cs] = resid[:, cs] + (z + bd_ref[:, cs])
            return 0

        lax.fori_loop(0, width // tile, down_step, 0)
        if k:
            z_copies[k - 1].start()
    for copy in z_copies:
        copy.wait_recv()
    total = resid[...]
    for n in range(len(offs)):
        total = total + zrecv[n].astype(F32)
    out_ref[...] = total.astype(out_ref.dtype)
    for copy in sends + z_copies:
        copy.wait_send()


def params(collective_id):
    return pltpu.CompilerParams(collective_id=collective_id, has_side_effects=True, vmem_limit_bytes=60 * 1024 * 1024)


def solution(mesh):
    tp = mesh.shape["tp"]
    side = math.isqrt(tp // CORES)
    col_groups = [[(y * side + x) * CORES + c for y in range(side) for c in range(CORES)] for x in range(side)]
    col = side * CORES
    near = side - 1

    def local_forward(x_local, ln1_gain, ln1_bias, ln2_gain, ln2_bias, w_qkv, w_out, b_out, w_up, b_up, w_down, b_down):
        _, share, width = x_local.shape
        layers, _, three, _, dim = w_qkv.shape
        scale = 1.0 / math.sqrt(dim)
        hidden = w_up.shape[2]
        wq_t = jnp.transpose(w_qkv, (0, 2, 3, 4, 1)).reshape(layers, three * dim, width)
        bup_all = lax.all_gather(b_up, "tp", axis=0, axis_index_groups=col_groups)
        gathered = []
        for layer in range(layers):
            gathered.append((
                lax.all_gather(wq_t[layer], "tp", axis=0, axis_index_groups=col_groups),
                lax.all_gather(w_out[layer].reshape(dim, width), "tp", axis=0),
                lax.all_gather(w_up[layer], "tp", axis=0, axis_index_groups=col_groups),
                lax.all_gather(w_down[layer], "tp", axis=0, axis_index_groups=col_groups),
            ))
        resid = x_local[0]
        for layer in range(layers):
            gq, go, gu, gd = gathered[layer]
            qkv = pl.pallas_call(
                functools.partial(qkv_kernel, side),
                out_shape=jax.ShapeDtypeStruct((tp, three * dim, share), BF16),
                in_specs=[VMEM, VMEM, VMEM, HBM],
                out_specs=VMEM,
                scratch_shapes=[
                    pltpu.VMEM((col, three * dim, width), BF16),
                    pltpu.VMEM((side, share, width), BF16),
                    pltpu.VMEM((side, col, three * dim, share), BF16),
                    DMA, DMA((near,)), DMA((near,)), DMA((side, col)), DMA((side, col)),
                ],
                compiler_params=params(0),
                cost_estimate=pl.CostEstimate(flops=20_000_000_000, bytes_accessed=10_000_000, transcendentals=0),
                name=f"qkv{layer}",
            )(resid, ln1_gain[layer : layer + 1], ln1_bias[layer : layer + 1], gq)
            o = pl.pallas_call(
                functools.partial(attention_kernel, side, scale, 4 * share),
                out_shape=jax.ShapeDtypeStruct((tp, dim, share), BF16),
                in_specs=[VMEM],
                out_specs=VMEM,
                scratch_shapes=[pltpu.VMEM((tp, dim, share), BF16), DMA((tp,)), DMA((tp,))],
                compiler_params=params(1),
                cost_estimate=pl.CostEstimate(flops=20_000_000_000, bytes_accessed=10_000_000, transcendentals=0),
                name=f"attention{layer}",
            )(qkv)
            last = layer == layers - 1
            resid = pl.pallas_call(
                functools.partial(mlp_kernel, side),
                out_shape=jax.ShapeDtypeStruct((share, width), BF16 if last else F32),
                in_specs=[VMEM] * 7 + [HBM] * 3,
                out_specs=VMEM,
                scratch_shapes=[
                    pltpu.VMEM((tp * dim, width), BF16),
                    pltpu.VMEM((col, width, hidden), BF16),
                    pltpu.VMEM((col * hidden, width), BF16),
                    pltpu.VMEM((side, share, width), BF16),
                    pltpu.VMEM((share, col * hidden), BF16),
                    pltpu.VMEM((near, share, width), BF16),
                    pltpu.VMEM((near, share, width), BF16),
                    pltpu.VMEM((share, width), F32),
                    DMA((3,)), DMA((near,)), DMA((near,)), DMA((near,)), DMA((near,)),
                ],
                compiler_params=params(2),
                cost_estimate=pl.CostEstimate(flops=30_000_000_000, bytes_accessed=30_000_000, transcendentals=0),
                name=f"mlp{layer}",
            )(resid, o, b_out[layer : layer + 1], ln2_gain[layer : layer + 1], ln2_bias[layer : layer + 1],
              bup_all[:, layer][:, None], b_down[layer : layer + 1], go.reshape(tp * dim, width), gu, gd.reshape(col * hidden, width))
        return resid[None]

    rows_spec = P("dp", "tp", None)
    in_specs = (rows_spec, P(), P(), P(), P(), P(None, None, None, "tp", None), P(None, "tp", None, None), P(), P(None, None, "tp"), P(None, "tp"), P(None, "tp", None), P())
    return jax.shard_map(local_forward, mesh=mesh, in_specs=in_specs, out_specs=rows_spec, check_vma=False)
```

time: 599 us -> 492 us (0.82); the launches traced: 590 us -> 491 us
  Pallas kernels: 56.3 us -> 274 us
  waiting for transfers between devices: 312 us -> 167 us
  matrix products: 58 us -> 0 us
  blocking collectives: 73.6 us -> 22.9 us
  local copies, waits for them, and re-layouts: 42.5 us -> 12.7 us
  starting transfers between devices: 20.4 us -> 0.45 us
  other arithmetic: 12.4 us -> 0 us
    pallas_call x2 -> x6, Pallas kernels: 56.3 us -> 274 us  [the longest x2 114 us: local_forward(): pl.pallas_call(functools.partial(mlp_kernel, side), out_shape=jax.ShapeDt...]
    all_gather x4 -> x0, waiting for transfers between devices: 107 us -> none  [local_forward(): lax.all_gather(normed, 'tp', axis=0, axis_index_groups=row_groups, tiled=...]
    all_gather x2, waiting for transfers between devices: 0.02 us -> 105 us  [local_forward(): lax.all_gather(w_out[layer].reshape(dim, width), 'tp', axis=0)]
    all_to_all x4 -> x0, waiting for transfers between devices: 70.3 us -> none  [the longest x1 25.2 us: local_forward(): lax.all_to_all(z.reshape(side, share, width), 'tp', 0, 0, axis_index_grou...]
    dot_general x6 -> x0, matrix products: 58 us -> none  [the longest x2 33.5 us: local_forward(): jnp.einsum('sgf,gfd->sd', act, gd, preferred_element_type=F32).astype(BF16)]
    all_to_all x2 -> x0, blocking collectives: 57.3 us -> none  [the longest x1 28.9 us: local_forward(): lax.all_to_all(z.reshape(side, share, width), 'tp', 0, 0, axis_index_grou...]
    all_gather x2, waiting for transfers between devices: 87.5 us -> 51.1 us  [local_forward(): lax.all_gather(w_down[layer], 'tp', axis=0, axis_index_groups=col_groups)]
    all_gather x2, waiting for transfers between devices: 40.4 us -> 8.57 us  [local_forward(): lax.all_gather(wq_t[layer], 'tp', axis=0, axis_index_groups=col_groups)]
  transfers between devices with their start and end apart: 16 -> 8, of which waited for: 12 -> 5; matrix products, arithmetic and copies ran while one was open for 15% -> 2% of each run, Pallas kernels for 10% -> 44%
where the time goes in v2:
time: 492 us; the launch traced here: 491 us
  Pallas kernels  274 us (56%)
  waiting for transfers between devices  167 us (34%)
  blocking collectives  22.9 us (5%)
  between operations  13.7 us (3%)
  local copies, waits for them, and re-layouts  12.7 us (3%)
    pallas_call x2, Pallas kernels, local_forward(): pl.pallas_call(functools.partial(mlp_kernel, side), out_shape=jax.ShapeDt...  114 us
    all_gather x2, waiting for transfers between devices, local_forward(): lax.all_gather(w_out[layer].reshape(dim, width), 'tp', axis=0)  105 us
    pallas_call x2, Pallas kernels, local_forward(): pl.pallas_call(functools.partial(qkv_kernel, side), out_shape=jax.ShapeDt...  96.9 us
    pallas_call x2, Pallas kernels, local_forward(): pl.pallas_call(functools.partial(attention_kernel, side, scale, 4 * share...  63.3 us
    all_gather x2, waiting for transfers between devices, local_forward(): lax.all_gather(w_down[layer], 'tp', axis=0, axis_index_groups=col_groups)  51.1 us
    all_gather x1, blocking collectives, local_forward(): bup_all = lax.all_gather(b_up, 'tp', axis=0, axis_index_groups=col_groups)  22.9 us
  transfers between devices with their start and end apart: 8, of which 5 were waited for; matrix products, arithmetic and copies ran while one was open for 2% of the time, Pallas kernels for 44%

profile of v2, /device:TPU:97, one launch (start us, length us, event | category | flops | bytes accessed | tf_op | source)
XLA Modules:
  0.0 490.9 jit_solution(10202936127907185700)
XLA Ops:
  6.6 2.9 fusion.2
  9.5 0.1 all-gather.15.cloned.1.call-start
  9.5 3.0 fusion.1
  12.7 0.1 all-gather.17.cloned.1.call-start
  12.8 1.5 fusion
  14.3 0.1 all-gather.25.cloned.1.call-start
  14.4 0.8 fusion.3
  15.3 0.1 all-gather.19.cloned.1.call-start
  15.4 0.6 all-gather.19.cloned.1.call-update
  16.0 0.1 all-gather.21.cloned.1.call-start
  16.0 0.6 all-gather.21.cloned.1.call-update
  16.6 0.1 all-gather.23.cloned.1.call-start
  16.7 0.7 all-gather.23.cloned.1.call-update
  17.4 0.1 all-gather.27.cloned.1.call-start
  17.5 0.7 all-gather.27.cloned.1.call-update
  18.2 22.9 %all-gather.3 = f32[8,2,256]{2,1,0:T(2,128)S(1)} all-gather(f32[1,2,256]{2,1,0:T(2,128)S(1)} %bitcast.14), channel_id=2, replica_groups={{0,1,8,9,16,17,24,25},{2,3,10,11,18,19,26,27},{4,5,12,13,20,21,28,29},{..., dimensions={0}, use_global_device_ids=true | all-gather | bytes 18432 | tf_op jit(solution)/shard_map/all_gather | solution.py:246
  41.1 0.6 fusion.5
  41.8 0.6 fusion.9
  42.4 0.6 fusion.4
  43.1 0.6 fusion.7
  43.7 8.6 %all-gather.13.cloned.1.call-done.w_hbm = bf16[8,192,2048]{2,1,0:T(8,128)(2,1)} async-done(((bf16[1,192,2048]{2,1,0:T(8,128)(2,1)}), bf16[8,192,2048]{2,1,0:T(8,128)(2,1)}) %all-gather.13.cloned.1.call-update) | async-done | bytes 6291472 | tf_op jit(solution)/shard_map/all_gather | solution.py:250
  52.2 48.6 %qkv0.1.qkv_ref = bf16[32,192,128]{2,1,0:T(8,128)(2,1)} custom-call(bf16[128,2048]{1,0:T(8,128)(2,1)} %bitcast.19, f32[1,2048]{1,0:T(1,128)} %get-tuple-element.27.gain_ref, f32[1,2048]{1,0:T(1,128)} %get-tuple-element.24.shift_ref, bf16[8,192,2048]{2,1,0:T(8,128)(2,1)} %all-gather.13.cloned.1.call-done.w_hbm), custom_call_target="tpu_custom_call" | custom-call | flops 20000000000 | bytes 10000000 | tf_op jit(solution)/shard_map/qkv0/pallas_call | solution.py:258
  100.8 31.1 %attention0.1.o_ref = bf16[32,64,128]{2,1,0:T(8,128)(2,1)} custom-call(bf16[32,192,128]{2,1,0:T(8,128)(2,1)} %qkv0.1.qkv_ref), custom_call_target="tpu_custom_call" | custom-call | flops 20000000000 | bytes 10000000 | tf_op jit(solution)/shard_map/attention0/pallas_call | solution.py:273
  131.9 33.1 %all-gather.17.cloned.1.call-done = bf16[8,256,2048]{2,1,0:T(8,128)(2,1)} async-done(((bf16[1,256,2048]{2,1,0:T(8,128)(2,1)}), bf16[8,256,2048]{2,1,0:T(8,128)(2,1)}) %all-gather.17.cloned.1.call-update) | async-done | bytes 8388624 | tf_op jit(solution)/shard_map/all_gather | solution.py:253
  165.1 52.2 %all-gather.25.cloned.1.call-done = bf16[32,1,64,2048]{3,2,1,0:T(8,128)(2,1)} async-done(((bf16[1,1,64,2048]{3,2,1,0:T(8,128)(2,1)}), bf16[32,1,64,2048]{3,2,1,0:T(8,128)(2,1)}) %all-gather.25.cloned.1.call-update) | async-done | bytes 8388624 | tf_op jit(solution)/shard_map/all_gather | solution.py:251
  217.3 56.3 %mlp0.1.r_ref = f32[128,2048]{1,0:T(8,128)} custom-call(bf16[128,2048]{1,0:T(8,128)(2,1)} %bitcast.20, bf16[32,64,128]{2,1,0:T(8,128)(2,1)} %attention0.1.o_ref, f32[1,2048]{1,0:T(1,128)} %get-tuple-element.31.bo_ref, f32[1,2048]{1,0:T(1,128)} %get-tuple-element.20.gain_ref, f32[1,2048]{1,0:T(1,128)} %get-tuple-element.29.shift_ref, ...), custom_call_target="tpu_custom_call" | custom-call | flops 30000001024 | bytes 30000000 | tf_op jit(solution)/shard_map/mlp0/pallas_call | solution.py:284
  273.7 48.3 %qkv1.1.qkv_ref = bf16[32,192,128]{2,1,0:T(8,128)(2,1)} custom-call(f32[128,2048]{1,0:T(8,128)} %mlp0.1.r_ref, f32[1,2048]{1,0:T(1,128)} %get-tuple-element.28.gain_ref, f32[1,2048]{1,0:T(1,128)} %get-tuple-element.23.shift_ref, bf16[8,192,2048]{2,1,0:T(8,128)(2,1)} %all-gather.19.cloned.1.call-done.w_hbm), custom_call_target="tpu_custom_call" | custom-call | flops 20000000000 | bytes 10000000 | tf_op jit(solution)/shard_map/qkv1/pallas_call | solution.py:258
  322.0 32.2 %attention1.1.o_ref = bf16[32,64,128]{2,1,0:T(8,128)(2,1)} custom-call(bf16[32,192,128]{2,1,0:T(8,128)(2,1)} %qkv1.1.qkv_ref), custom_call_target="tpu_custom_call" | custom-call | flops 20000000000 | bytes 10000000 | tf_op jit(solution)/shard_map/attention1/pallas_call | solution.py:273
  354.2 17.9 %all-gather.23.cloned.1.call-done = bf16[8,256,2048]{2,1,0:T(8,128)(2,1)} async-done(((bf16[1,256,2048]{2,1,0:T(8,128)(2,1)}), bf16[8,256,2048]{2,1,0:T(8,128)(2,1)}) %all-gather.23.cloned.1.call-update) | async-done | bytes 8388624 | tf_op jit(solution)/shard_map/all_gather | solution.py:253
  372.2 52.5 %all-gather.27.cloned.1.call-done = bf16[32,1,64,2048]{3,2,1,0:T(8,128)(2,1)} async-done(((bf16[1,1,64,2048]{3,2,1,0:T(8,128)(2,1)}), bf16[32,1,64,2048]{3,2,1,0:T(8,128)(2,1)}) %all-gather.27.cloned.1.call-update) | async-done | bytes 8388624 | tf_op jit(solution)/shard_map/all_gather | solution.py:251
  424.7 57.5 %mlp1.1 = bf16[128,2048]{1,0:T(8,128)(2,1)} custom-call(f32[128,2048]{1,0:T(8,128)} %mlp0.1.r_ref, bf16[32,64,128]{2,1,0:T(8,128)(2,1)} %attention1.1.o_ref, f32[1,2048]{1,0:T(1,128)} %get-tuple-element.32.bo_ref, f32[1,2048]{1,0:T(1,128)} %get-tuple-element.19.gain_ref, f32[1,2048]{1,0:T(1,128)} %get-tuple-element.30.shift_ref, ...), custom_call_target="tpu_custom_call" | custom-call | flops 30000001024 | bytes 30000000 | tf_op jit(solution)/shard_map/mlp1/pallas_call | solution.py:284
  482.2 1.9 copy.14
  (26 shorter events, 0.3 us)
Async XLA Ops:
  6.5 6.2 %copy-start = (bf16[2,256,2048]{2,1,0:T(8,128)(2,1)S(1)}, bf16[2,256,2048]{2,1,0:T(8,128)(2,1)}, u32[]{:S(2)}) copy-start(bf16[2,256,2048]{2,1,0:T(8,128)(2,1)} %param.22) | copy-start | bytes 6291460
  6.5 45.7 %all-gather.13.cloned.1.call-start = ((), (), s32[]{:S(2)}) async-start(), calls=%async_computation | async-start | bytes 7077888 | tf_op jit(solution)/shard_map/all_gather | solution.py:250
  9.4 5.0 %copy-start.1 = (bf16[2,1,64,2048]{3,2,1,0:T(8,128)(2,1)S(1)}, bf16[2,1,64,2048]{3,2,1,0:T(8,128)(2,1)}, u32[]{:S(2)}) copy-start(bf16[2,1,64,2048]{3,2,1,0:T(8,128)(2,1)} %param.18) | copy-start | bytes 1572868
  9.5 122.4 %all-gather.15.cloned.1.call-start = ((), (), s32[]{:S(2)}) async-start(), calls=%async_computation.1 | async-start | bytes 9437184 | tf_op jit(solution)/shard_map/all_gather | solution.py:252
  12.6 5.7 %copy-start.8 = (f32[2,256]{1,0:T(2,128)S(1)}, f32[2,256]{1,0:T(2,128)}, u32[]{:S(2)}) copy-start(f32[2,256]{1,0:T(2,128)} %param.21) | copy-start | bytes 6148
  12.6 29.2 %copy-start.2 = (f32[2,2048]{1,0:T(2,128)S(1)}, f32[2,2048]{1,0:T(2,128)}, u32[]{:S(2)}) copy-start(f32[2,2048]{1,0:T(2,128)} %param.14) | copy-start | bytes 49156
  12.6 29.2 %copy-start.3 = (f32[2,2048]{1,0:T(2,128)S(1)}, f32[2,2048]{1,0:T(2,128)}, u32[]{:S(2)}) copy-start(f32[2,2048]{1,0:T(2,128)} %param.13) | copy-start | bytes 49156
  12.6 29.8 %copy-start.4 = (f32[2,2048]{1,0:T(2,128)S(1)}, f32[2,2048]{1,0:T(2,128)}, u32[]{:S(2)}) copy-start(f32[2,2048]{1,0:T(2,128)} %param.23) | copy-start | bytes 49156
  12.6 29.8 %copy-start.5 = (f32[2,2048]{1,0:T(2,128)S(1)}, f32[2,2048]{1,0:T(2,128)}, u32[]{:S(2)}) copy-start(f32[2,2048]{1,0:T(2,128)} %param.16) | copy-start | bytes 49156
  12.6 30.4 %copy-start.6 = (f32[2,2048]{1,0:T(2,128)S(1)}, f32[2,2048]{1,0:T(2,128)}, u32[]{:S(2)}) copy-start(f32[2,2048]{1,0:T(2,128)} %param.15) | copy-start | bytes 49156
  12.6 30.4 %copy-start.7 = (f32[2,2048]{1,0:T(2,128)S(1)}, f32[2,2048]{1,0:T(2,128)}, u32[]{:S(2)}) copy-start(f32[2,2048]{1,0:T(2,128)} %param.19) | copy-start | bytes 49156
  12.7 152.4 %all-gather.17.cloned.1.call-start = ((), (), s32[]{:S(2)}) async-start(), calls=%async_computation.2 | async-start | bytes 9437184 | tf_op jit(solution)/shard_map/all_gather | solution.py:253
  14.3 203.0 %all-gather.25.cloned.1.call-start = ((), (), s32[]{:S(2)}) async-start(), calls=%async_computation.6 | async-start | bytes 8650752 | tf_op jit(solution)/shard_map/all_gather | solution.py:251
  15.3 258.3 %all-gather.19.cloned.1.call-start = ((), (), s32[]{:S(2)}) async-start(), calls=%async_computation.3 | async-start | bytes 7077888 | tf_op jit(solution)/shard_map/all_gather | solution.py:250
  16.0 338.2 %all-gather.21.cloned.1.call-start = ((), (), s32[]{:S(2)}) async-start(), calls=%async_computation.4 | async-start | bytes 9437184 | tf_op jit(solution)/shard_map/all_gather | solution.py:252
  16.6 355.5 %all-gather.23.cloned.1.call-start = ((), (), s32[]{:S(2)}) async-start(), calls=%async_computation.5 | async-start | bytes 9437184 | tf_op jit(solution)/shard_map/all_gather | solution.py:253
  17.4 407.3 %all-gather.27.cloned.1.call-start = ((), (), s32[]{:S(2)}) async-start(), calls=%async_computation.7 | async-start | bytes 8650752 | tf_op jit(solution)/shard_map/all_gather | solution.py:251
Sparse Core Ops, SparseCore 0:
  9.6 42.5 all-gather.12
  53.8 64.3 all-gather.14
  119.8 45.1 all-gather.16
  167.0 50.2 all-gather.24
  218.7 37.8 all-gather.18
  258.1 63.7 all-gather.20
  323.6 48.5 all-gather.22
  374.2 50.4 all-gather.26

commit v3 on v0

v3 whole, which is shorter than its diff:
```python
import functools
import math
import jax
import jax.numpy as jnp
from jax import lax
from jax.experimental import pallas as pl
from jax.experimental.pallas import tpu as pltpu
from jax.sharding import PartitionSpec as P

F32 = jnp.float32
BF16 = jnp.bfloat16
CORES = 2
NN = (((1,), (0,)), ((), ()))
NT = (((1,), (1,)), ((), ()))
TN = (((0,), (0,)), ((), ()))
MESH = pl.DeviceIdType.MESH
VMEM = pl.BlockSpec(memory_space=pltpu.VMEM)
HBM = pl.BlockSpec(memory_space=pl.ANY)
DMA = pltpu.SemaphoreType.DMA


def place(side):
    me = lax.axis_index("tp")
    return me, me // (side * CORES), (me // CORES) % side, me % CORES


def index_of(side, y, x, c):
    return (y * side + x) * CORES + c


def dev(index):
    return {"tp": index}


def remote(src, dst, send_sem, recv_sem, index):
    return pltpu.make_async_remote_copy(src_ref=src, dst_ref=dst, send_sem=send_sem, recv_sem=recv_sem, device_id=dev(index), device_id_type=MESH)


def enter(indices):
    barrier = pltpu.get_barrier_semaphore()
    for index in indices:
        pl.semaphore_signal(barrier, inc=1, device_id=dev(index), device_id_type=MESH)
    pl.semaphore_wait(barrier, len(indices))


def norm(resid, gain, shift):
    row_mean = jnp.mean(resid, axis=-1, keepdims=True)
    centered = resid - row_mean
    variance = jnp.mean(centered * centered, axis=-1, keepdims=True)
    return (centered * lax.rsqrt(variance + 1e-5) * gain + shift).astype(BF16)


def ring_order(side):
    return sorted(range(1, side), key=lambda off: min(off, side - off))


class Gather:
    def __init__(self, ring, src, slot, half, recv, send, partner):
        self.prev, self.next, self.back, self.here, self.fwd, self.far = ring
        self.src, self.slot, self.half, self.recv, self.send, self.partner = src, slot, half, recv, send, partner

    def start(self):
        dst = self.slot(self.here, 0)
        remote(self.src, dst, self.send, self.recv.at[0], self.next).start()
        remote(self.src, dst, self.send, self.recv.at[1], self.prev).start()
        if self.partner is not None:
            remote(self.src, dst, self.send, self.recv.at[4], self.partner).start()

    def landed(self, ref, n):
        remote(ref, ref, self.send, self.recv.at[n], self.next).wait_recv()

    def share(self, pos, n):
        if self.partner is not None:
            ref = self.slot(pos, 0)
            remote(ref, ref, self.send, self.recv.at[n], self.partner).start()

    def relay(self):
        for n, pos, to in ((0, self.back, self.next), (1, self.fwd, self.prev)):
            self.landed(self.slot(pos, 0), n)
            ref = self.half(pos, n)
            remote(ref, ref, self.send, self.recv.at[2 + n], to).start()
            self.share(pos, 5 + n)

    def last(self):
        self.landed(self.half(self.far, 0), 2)
        self.landed(self.half(self.far, 1), 3)
        self.share(self.far, 7)

    def finish(self):
        if self.partner is not None:
            for n, pos in enumerate((self.here, self.back, self.fwd, self.far)):
                self.landed(self.slot(pos, 1), 4 + n)

    def drain(self, whole):
        ref = whole(7 if self.partner is not None else 3)
        remote(ref, ref, self.send, self.recv.at[0], self.next).wait_send()


def decoder_kernel(side, layers, x_ref, ln1g, ln1b, ln2g, ln2b, bo_ref, bu_ref, bd_ref, wq_in, wo_in, wu_in, wd_in,
                   out_ref, gq, go, gu, gd,
                   wq, wo, wu, wd, h1, h2, qkv, qsend, oall, osend, ubuf, zsend, zrecv, resid, bup,
                   g_recv, g_send, h_send, h_recv, q_sem, o_sem, z_send, z_recv, b_sem, l_sem):
    me, y, x, c = place(side)
    col = side * CORES
    tp = side * col
    near = side - 1
    mine = y * CORES + c
    offs = ring_order(side)
    share, width = x_ref.shape
    dim = oall.shape[2]
    hidden = wu.shape[2]
    tile = 256
    partner = index_of(side, y, x, 1 - c)

    def in_col(m):
        return index_of(side, m // CORES, x, m % CORES)

    def ring(at, p):
        back, fwd, far = (p + side - 1) % side, (p + 1) % side, (p + 2) % side
        return at(back), at(fwd), back, p, fwd, far

    along_y = ring(lambda p: index_of(side, p, x, c), y)
    along_x = ring(lambda p: index_of(side, y, p, c), x)

    def weights(layer, n, src, buf):
        rows = buf.shape[2] // 2

        def slot(pos, other):
            return buf.at[layer, pos * CORES + (c if other == 0 else 1 - c)]

        def half(pos, n):
            return buf.at[layer, pos * CORES + c, pl.ds(n * rows, rows)]

        return Gather(along_y, src.at[layer], slot, half, g_recv.at[layer, n], g_send.at[layer, n], partner)

    def w_out_y(layer):
        here = x * CORES + c

        def slot(pos, other):
            return go.at[layer, here, pl.ds(pl.multiple_of(pos * dim, dim), dim)]

        def half(pos, n):
            return go.at[layer, here, pl.ds(pl.multiple_of(pos * dim + n * (dim // 2), dim // 2), dim // 2)]

        return Gather(along_y, wo_in.at[layer], slot, half, g_recv.at[layer, 3], g_send.at[layer, 3], None)

    def w_out_x(layer):
        rows = go.shape[2] // 2

        def slot(pos, other):
            return go.at[layer, pos * CORES + (c if other == 0 else 1 - c)]

        def half(pos, n):
            return go.at[layer, pos * CORES + c, pl.ds(n * rows, rows)]

        return Gather(along_x, slot(x, 0), slot, half, g_recv.at[layer, 4], g_send.at[layer, 4], partner)

    q_job = [weights(layer, 0, wq_in, gq) for layer in range(layers)]
    u_job = [weights(layer, 1, wu_in, gu) for layer in range(layers)]
    d_job = [weights(layer, 2, wd_in, gd) for layer in range(layers)]
    oy_job = [w_out_y(layer) for layer in range(layers)]
    ox_job = [w_out_x(layer) for layer in range(layers)]

    def load_rest(buf, dst, layer, n):
        return [pltpu.make_async_copy(buf.at[layer, (mine + d) % col], dst.at[(mine + d) % col], l_sem.at[n, d]) for d in range(1, col)]

    def own_load(src, dst, layer, n):
        return pltpu.make_async_copy(src.at[layer], dst.at[mine], l_sem.at[n, 0])

    def begin(copies):
        for copy in copies:
            copy.start()

    def end(copies):
        for copy in copies:
            copy.wait()

    enter([(me + d) % tp for d in range(1, tp)])
    q_job[0].start()
    for layer in range(layers):
        out_copy(wo_in, oy_job, layer, y, l_sem).start()
    for d in range(1, col):
        remote(bu_ref, bup.at[mine], b_sem.at[0], b_sem.at[1], in_col((mine + d) % col)).start()
    bup[mine] = bu_ref[...]
    resid[...] = x_ref[...].astype(F32)

    def send_h(layer, which, buf):
        peers = [index_of(side, y, (x + off) % side, c) for off in offs]
        return [remote(buf.at[layer, x], buf.at[layer, x], h_send.at[layer, which, n], h_recv.at[layer, which, n], peers[n]) for n in range(near)]

    for layer in range(layers):
        first, final = layer == 0, layer == layers - 1
        row = slice(layer, layer + 1)
        h1[layer, x] = norm(resid[...], ln1g[row, :], ln1b[row, :])
        h_copies = send_h(layer, 0, h1)
        begin(h_copies)
        if first:
            loads = [own_load(wq_in, wq, layer, 0)] + load_rest(gq, wq, layer, 0)
            loads[0].start()
            oy_job[0].start()
            q_job[0].relay()
            q_job[0].last()
            q_job[0].finish()
            begin(loads[1:])
            end(loads)

        def q_copy(k, d, xk):
            return remote(qsend.at[k, d], qkv.at[layer, index_of(side, y, xk, c)], q_sem.at[layer, 0], q_sem.at[layer, 1], in_col((mine + d) % col))

        for k in range(side):
            xk = (x - ([0] + offs)[k] + side) % side
            if k:
                h_copies[k - 1].wait_recv()

            def q_part(n, _):
                d = (n + 1) % col
                part = lax.dot_general(wq[(mine + d) % col], h1[layer, xk], NT, preferred_element_type=F32).astype(BF16)

                @pl.when(d != 0)
                def _():
                    qsend[k, d] = part
                    q_copy(k, d, xk).start()

                @pl.when(d == 0)
                def _():
                    qkv[layer, index_of(side, y, xk, c)] = part

                return 0

            lax.fori_loop(0, col, q_part, 0)
        oy_job[layer].relay()
        oy_job[layer].last()
        out_copy(wo_in, oy_job, layer, y, l_sem).wait()
        ox_job[layer].start()
        if first:
            u_job[layer].start()
        else:
            u_job[layer].relay()
            d_job[layer].start()
        moved = qkv.at[layer, pl.ds(0, side * (col - 1))]
        everything_qkv = remote(moved, moved, q_sem.at[layer, 0], q_sem.at[layer, 1], me)
        everything_qkv.wait_recv()

        def hook():
            ox_job[layer].relay()
            if first:
                u_job[layer].relay()
            else:
                u_job[layer].last()

        attend(side, layer, me, c, x, y, qkv, oall, osend, o_sem, hook)

        if first:
            d_job[layer].start()
        ox_job[layer].last()
        if first:
            u_job[layer].last()
        else:
            d_job[layer].relay()
        moved = oall.at[layer, pl.ds(0, tp - 1)]
        everything_o = remote(moved, moved, o_sem.at[layer, 0], o_sem.at[layer, 1], me)
        ox_job[layer].finish()
        load_o = pltpu.make_async_copy(go.at[layer], wo, l_sem.at[1, 0])
        load_o.start()
        load_u = [own_load(wu_in, wu, layer, 2)] + load_rest(gu, wu, layer, 2)
        load_d = [own_load(wd_in, wd, layer, 3)] + load_rest(gd, wd, layer, 3)
        begin([load_u[0], load_d[0]])
        everything_o.wait_recv()
        load_o.wait()
        o_t = oall[layer].reshape(tp * dim, share)

        def out_step(n, _):
            cs = pl.ds(pl.multiple_of(n * tile, tile), tile)
            w = wo[:, :, cs].reshape(tp * dim, tile)
            resid[:, cs] = resid[:, cs] + (lax.dot_general(o_t, w, TN, preferred_element_type=F32) + bo_ref[row, cs])
            return 0

        lax.fori_loop(0, width // tile, out_step, 0)
        h2[layer, x] = norm(resid[...], ln2g[row, :], ln2b[row, :])
        g_copies = send_h(layer, 1, h2)
        begin(g_copies)
        u_job[layer].finish()
        begin(load_u[1:])
        if first:
            moved = bup.at[pl.ds(0, col - 1)]
            remote(moved, moved, b_sem.at[0], b_sem.at[1], me).wait()
        else:
            d_job[layer].last()
        end(load_u)

        def chunk(k):
            return (x - ([0] + offs)[k] + side) % side

        def up(k):
            if k:
                g_copies[k - 1].wait_recv()

            def up_step(g, _):
                pre = lax.dot_general(h2[layer, chunk(k)], wu[g], NN, preferred_element_type=F32) + bup[g, row, :]
                ubuf[k, :, pl.ds(pl.multiple_of(g * hidden, 128), hidden)] = jax.nn.gelu(pre, approximate=True).astype(BF16)
                return 0

            lax.fori_loop(0, col, up_step, 0)

        z_copies = [remote(zsend.at[n], zrecv.at[layer, n], z_send.at[layer, n], z_recv.at[layer, n], index_of(side, y, chunk(n + 1), c)) for n in range(near)]

        def down(k):
            def down_step(n, _):
                cs = pl.ds(pl.multiple_of(n * tile, tile), tile)
                w = wd[:, :, cs].reshape(col * hidden, tile)
                z = lax.dot_general(ubuf[k], w, NN, preferred_element_type=F32)
                if k:
                    zsend[k - 1, :, cs] = z.astype(BF16)
                else:
                    resid[:, cs] = resid[:, cs] + (z + bd_ref[row, cs])
                return 0

            lax.fori_loop(0, width // tile, down_step, 0)
            if k:
                z_copies[k - 1].start()

        up(0)
        if first:
            d_job[layer].relay()
            if not final:
                q_job[layer + 1].start()
                oy_job[layer + 1].start()
            for k in range(1, side):
                up(k)
                if k == near - 1:
                    d_job[layer].last()
            d_job[layer].finish()
            begin(load_d[1:])
            end(load_d)
            for k in range(1, side):
                down(k)
            if not final:
                q_job[layer + 1].relay()
                q_job[layer + 1].last()
                u_job[layer + 1].start()
            down(0)
        else:
            if not final:
                q_job[layer + 1].start()
                oy_job[layer + 1].start()
            d_job[layer].finish()
            begin(load_d[1:])
            end(load_d)
            down(0)
            for k in range(1, side):
                up(k)
                down(k)
            if not final:
                q_job[layer + 1].relay()
                q_job[layer + 1].last()
                u_job[layer + 1].start()
        if not final:
            q_job[layer + 1].finish()
            loads = [own_load(wq_in, wq, layer + 1, 0)] + load_rest(gq, wq, layer + 1, 0)
            begin(loads)
        for copy in z_copies:
            copy.wait_recv()
        total = resid[...]
        for n in range(near):
            total = total + zrecv[layer, n].astype(F32)
        if final:
            out_ref[...] = total.astype(BF16)
        else:
            resid[...] = total
            end(loads)
        everything_qkv.wait_send()
        everything_o.wait_send()
        for copy in h_copies + g_copies + z_copies:
            copy.wait_send()
    for layer in range(layers):
        q_job[layer].drain(lambda n: gq.at[layer, pl.ds(0, n)])
        u_job[layer].drain(lambda n: gu.at[layer, pl.ds(0, n)])
        d_job[layer].drain(lambda n: gd.at[layer, pl.ds(0, n)])
        ox_job[layer].drain(lambda n: go.at[layer, pl.ds(0, n)])
        oy_job[layer].drain(lambda n: go.at[layer, 0, pl.ds(0, n * dim)])


def out_copy(wo_in, oy_job, layer, y, l_sem):
    return pltpu.make_async_copy(wo_in.at[layer], oy_job[layer].slot(y, 0), l_sem.at[4, layer])


def attend(side, layer, me, c, x, y, qkv, oall, osend, o_sem, hook):
    _, tp, three_dim, share = qkv.shape
    dim = three_dim // 3
    per = 4
    block = per * share
    c2 = math.log2(math.e) / math.sqrt(dim)
    rows = lax.broadcasted_iota(jnp.int32, (block, block), 0)
    cols = lax.broadcasted_iota(jnp.int32, (block, block), 1)
    slot = (x * CORES + c) * side + y
    steps = tp // per

    def part(i, which):
        return jnp.concatenate([qkv[layer, i * per + n, which * dim : (which + 1) * dim, :] for n in range(per)], axis=1)

    def q_step(i, _):
        @pl.when(i == steps - 1)
        def _():
            hook()

        q = part(i, 0).T

        def scores(j):
            return lax.dot_general(q, part(j, 1), NN, preferred_element_type=F32)

        def update(s, j, carry):
            m, l, acc = carry
            m_new = jnp.maximum(m, jnp.max(s, axis=-1, keepdims=True))
            p = jnp.exp2(s * c2 - m_new * c2)
            alpha = jnp.exp2((m - m_new) * c2)
            acc = acc * alpha + lax.dot_general(p.astype(BF16), part(j, 2), NT, preferred_element_type=F32)
            return m_new, l * alpha + jnp.sum(p, axis=-1, keepdims=True), acc

        init = (jnp.full((block, 1), -1e30, F32), jnp.zeros((block, 1), F32), jnp.zeros((block, dim), F32))
        carry = lax.fori_loop(0, i, lambda j, carry: update(scores(j), j, carry), init)
        _, l, acc = update(jnp.where(rows >= cols, scores(i), -1e30), i, carry)
        o_t = (acc / l).T.astype(BF16)
        for n in range(per):
            d = (i * per + n - me + tp) % tp
            piece = o_t[:, n * share : (n + 1) * share]

            @pl.when(d != 0)
            def _():
                osend[d] = piece
                remote(osend.at[d], oall.at[layer, slot], o_sem.at[layer, 0], o_sem.at[layer, 1], i * per + n).start()

            @pl.when(d == 0)
            def _():
                oall[layer, slot] = piece

        return 0

    lax.fori_loop(0, steps, q_step, 0)


def solution(mesh):
    tp = mesh.shape["tp"]
    side = math.isqrt(tp // CORES)
    col = side * CORES
    near = side - 1

    def local_forward(x_local, ln1_gain, ln1_bias, ln2_gain, ln2_bias, w_qkv, w_out, b_out, w_up, b_up, w_down, b_down):
        _, share, width = x_local.shape
        layers, _, three, _, dim = w_qkv.shape
        hidden = w_up.shape[2]
        wq_t = jnp.transpose(w_qkv, (0, 2, 3, 4, 1)).reshape(layers, three * dim, width)
        hbm = lambda *shape: jax.ShapeDtypeStruct(shape, BF16)
        vmem = lambda *shape: pltpu.VMEM(shape, BF16)
        y = pl.pallas_call(
            functools.partial(decoder_kernel, side, layers),
            out_shape=(
                hbm(share, width), hbm(layers, col, three * dim, width), hbm(layers, col, side * dim, width),
                hbm(layers, col, width, hidden), hbm(layers, col, hidden, width),
            ),
            in_specs=[VMEM] * 8 + [HBM] * 4,
            out_specs=(VMEM, HBM, HBM, HBM, HBM),
            scratch_shapes=[
                vmem(col, three * dim, width), vmem(col, side * dim, width), vmem(col, width, hidden), vmem(col, hidden, width),
                vmem(layers, side, share, width), vmem(layers, side, share, width),
                vmem(layers, tp, three * dim, share), vmem(side, col, three * dim, share),
                vmem(layers, tp, dim, share), vmem(tp, dim, share),
                vmem(side, share, col * hidden),
                vmem(near, share, width), vmem(layers, near, share, width),
                pltpu.VMEM((share, width), F32), pltpu.VMEM((col, layers, hidden), F32),
                DMA((layers, 5, 8)), DMA((layers, 5)), DMA((layers, 2, near)), DMA((layers, 2, near)),
                DMA((layers, 2)), DMA((layers, 2)), DMA((layers, near)), DMA((layers, near)), DMA((2,)), DMA((5, 8)),
            ],
            compiler_params=pltpu.CompilerParams(collective_id=0, has_side_effects=True, vmem_limit_bytes=63 * 1024 * 1024),
            name="decoder",
        )(x_local[0], ln1_gain, ln1_bias, ln2_gain, ln2_bias, b_out, b_up, b_down, wq_t, w_out.reshape(layers, dim, width), w_up, w_down)[0]
        return y[None]

    rows_spec = P("dp", "tp", None)
    in_specs = (rows_spec, P(), P(), P(), P(), P(None, None, None, "tp", None), P(None, "tp", None, None), P(), P(None, None, "tp"), P(None, "tp"), P(None, "tp", None), P())
    return jax.shard_map(local_forward, mesh=mesh, in_specs=in_specs, out_specs=rows_spec, check_vma=False)
```

time: 1440 us -> 334 us (0.23)
  waiting for transfers between devices: 714 us -> 0 us
  blocking collectives: 415 us -> 0 us
  Pallas kernels: 0 us -> 332 us
  matrix products: 196 us -> 0 us
  other arithmetic: 73.9 us -> 0 us
    all_to_all x2 -> x0, blocking collectives: 415 us -> none  [scatter_rows(): received = lax.all_to_all(pieces, 'tp', 1, 1, tiled=True)]
    all_to_all x2 -> x0, waiting for transfers between devices: 405 us -> none  [scatter_rows(): received = lax.all_to_all(pieces, 'tp', 1, 1, tiled=True)]
    pallas_call x0 -> x1, Pallas kernels: none -> 332 us  [local_forward(): pl.pallas_call(functools.partial(decoder_kernel, side, layers), out_shape...]
    all_gather x4 -> x0, waiting for transfers between devices: 309 us -> none  [the longest x2 156 us: local_forward(): gathered = lax.all_gather(normed, 'tp', axis=1, tiled=True)]
    dot_general x6 -> x0, matrix products: 177 us -> none  [the longest x2 79.7 us: local_forward(): jnp.einsum('cirf,ife->cre', attn_heads, w_out[layer], preferred_element_t...]
    reduce_sum x14 -> x0, other arithmetic: 67.1 us -> none  [the longest x2 43.5 us: local_forward(): jax.nn.softmax(jnp.where(causal, scores, -1e+30), axis=-1)]
    unnamed x2 -> x0, matrix products: 18.6 us -> none
  transfers between devices with their start and end apart: 6 -> 0, of which waited for: 6 -> 0; matrix products, arithmetic and copies ran while one was open for 0% -> 0% of each run, Pallas kernels for 0% -> 0%
where the time goes in v3:
time: 334 us
  Pallas kernels  332 us (99%)
    pallas_call x1, Pallas kernels, local_forward(): pl.pallas_call(functools.partial(decoder_kernel, side, layers), out_shape...  332 us

profile of v3, /device:TPU:97, one launch (start us, length us, event | category | flops | bytes accessed | tf_op | source)
XLA Modules:
  0.0 333.6 jit_solution(10618772380622685352)
XLA Ops:
  0.0 331.7 %decoder.1 = (bf16[128,2048]{1,0:T(8,128)(2,1)}, bf16[2,8,192,2048]{3,2,1,0:T(8,128)(2,1)}, bf16[2,8,256,2048]{3,2,1,0:T(8,128)(2,1)}, bf16[2,8,2048,256]{3,2,1,0:T(8,128)(2,1)}, bf16[2,8,256,2048]{3,2,1,0:T(8,128)(2,1)}) custom-call(bf16[128,2048]{1,0:T(8,128)(2,1)} %bitcast.7, f32[2,2048]{1,0:T(2,128)} %ln1g.1, f32[2,2048]{1,0:T(2,128)} %ln1b.1, ...), custom_call_target="tpu_custom_call" | custom-call | tf_op jit(solution)/shard_map/decoder/pallas_call | solution.py:454
  331.8 1.9 copy.14
